TPU v7x, 32 devices: a whole 2x2x4 slice. The times are simulated.
32 devices in a mesh: expert: 8 (over z, y), replica: 2 (over core), group: 2 (over x).
Axes of the slice: x: 2, y: 2, z: 4, core: 2. Of those that a mesh axis runs over, the one named last changes fastest.
Arguments:
- tokens: bfloat16 [1536, 4096], P('expert', 'group'), may hold values from -6 to 6
- expert_ids: int32 [1536, 8], P('expert'), may hold values from 0 to 127, all different within a row; in each aligned block of 192 rows (0 to 191, 192 to 383, ...) at most 15 rows name the same one
- route_gates: float32 [1536, 8], P('expert'), may hold values from 0.03 to 0.5
- member_order: int32 [8], replicated, may hold values from 0 to 7, each once
- teach_gate: bfloat16 [8, 1536, 4096], P('expert', 'replica', 'group'), may hold values from -0.09375 to 0.09375
- teach_up: bfloat16 [8, 1536, 4096], P('expert', 'replica', 'group'), may hold values from -0.09375 to 0.09375
- teach_down: bfloat16 [8, 1536, 4096], P('expert', 'replica', 'group'), may hold values from -0.15625 to 0.15625
- stud_gate: bfloat16 [8, 1536, 2048], P('expert', 'replica', 'group'), may hold values from -0.09375 to 0.09375
- stud_up: bfloat16 [8, 1536, 2048], P('expert', 'replica', 'group'), may hold values from -0.09375 to 0.09375
- stud_down: bfloat16 [8, 1536, 2048], P('expert', 'replica', 'group'), may hold values from -0.15625 to 0.15625
Outputs:
- residual: float32 [1536, 4096], P('expert', ('group', 'replica'))
- grad_gate: bfloat16 [8, 1536, 2048], P('expert', 'replica', 'group')
- grad_up: bfloat16 [8, 1536, 2048], P('expert', 'replica', 'group')
- grad_down: bfloat16 [8, 1536, 2048], P('expert', 'replica', 'group')
Inputs may be any that keep to these rules, and one draw needn't show every extreme that they name: `expert_ids`: each row names 8 different experts. Within each aligned block of 192 rows no expert is named by more than 15 rows. Only experts below 8 are in the window. `member_order`: every teacher expert of the window appears once.
All inputs are finite; a program needn't handle non-finite values.
Results may differ from a plain program's by a relative error of at most 0.025.
Values may be sent and summed in bfloat16 or wider, within the bound.
No kernel may reach another device: no remote copies, remote signals or barrier semaphores. Data moves between devices by JAX's collectives and lax.ppermute only.
A program may use at most 128 MiB of HBM per device.

v0:
```python
import jax
import jax.numpy as jnp
from jax import lax
from jax.experimental import pallas as pl
from jax.experimental.pallas import tpu as pltpu
from jax.sharding import PartitionSpec as P


SLOT = 16


BF16 = jnp.bfloat16
F32 = jnp.float32


def swap(block, axis):
    count = lax.axis_size(axis)
    return lax.ppermute(block, axis, [(place, place ^ 1) for place in range(count)])


def quad(diagonal, group, expert):
    count = 2 * lax.axis_size("expert")
    crossing = [(place, place ^ 3) for place in range(count)]
    diagonal = lax.ppermute(diagonal, ("expert", "group"), crossing)
    return diagonal, swap(group, "group"), swap(expert, "expert")


def exchange(block):
    return lax.all_to_all(block, "expert", split_axis=0, concat_axis=0, tiled=True)


def contract(left, right, dims):
    return lax.dot_general(left, right, ((dims[:1], dims[1:]), ((), ())), preferred_element_type=F32)


def call(body, outs, ins, scratch=(), smem=0, far=0, flops=0, limit=16, space=pltpu.VMEM):
    specs = [pl.BlockSpec(memory_space=pltpu.SMEM)] * smem
    specs += [pl.BlockSpec(memory_space=pltpu.HBM)] * far
    specs += [pl.BlockSpec(memory_space=pltpu.VMEM)] * (len(ins) - smem - far)
    moved = sum(x.size * x.dtype.itemsize for x in ins)
    spaces = [pltpu.HBM] * (smem + far) + [space] * (len(ins) - smem - far)
    placed = map(pltpu.with_memory_space_constraint, ins, spaces)
    return pl.pallas_call(
        body,
        out_shape=outs,
        in_specs=specs,
        out_specs=[pl.BlockSpec(memory_space=pltpu.VMEM)] * len(outs),
        scratch_shapes=scratch,
        cost_estimate=pl.CostEstimate(flops=flops, bytes_accessed=moved, transcendentals=0),
        compiler_params=pltpu.CompilerParams(vmem_limit_bytes=limit << 20),
    )(*placed)


def struct(dtype, *shape):
    return pltpu.VMEM(shape, dtype)


def result(dtype, *shape):
    return jax.ShapeDtypeStruct(shape, dtype)


def spread_members(order, source, target, to_slots):
    owners, _, narrow = target.shape if not to_slots else source.shape
    for dest in range(owners):
        columns = slice(dest % 2 * narrow, (dest % 2 + 1) * narrow)
        for member in range(2):
            start = pl.multiple_of(order[dest // 2 * 2 + member] * SLOT, SLOT)
            rows = slice(member * SLOT, (member + 1) * SLOT)
            if to_slots:
                target[pl.ds(start, SLOT), columns] = source[dest, rows, :]
            else:
                target[dest, rows, :] = source[pl.ds(start, SLOT), columns]


def loads_of(arrived, *pairs):
    loads = [pltpu.make_async_copy(far, near, arrived.at[at]) for at, (far, near) in enumerate(pairs)]
    for load in loads:
        load.start()
    return loads


def expert_hits(ids, slots):
    expert = lax.broadcasted_iota(jnp.int32, (slots, ids.shape[1]), 0) // SLOT
    return [ids[choice : choice + 1, :] == expert for choice in range(ids.shape[0])]


def route(order, gate_hbm, up_hbm, ids, tokens, send, select, gate_near, up_near, picked, arrived):
    loads = loads_of(arrived, (gate_hbm, gate_near), (up_hbm, up_near))
    owners, _, narrow = send.shape
    slots, count = select.shape
    slot = (lax.broadcasted_iota(jnp.int32, (slots, count), 0) % SLOT).astype(F32)
    member = jnp.zeros((slots, count), F32)
    for hit in expert_hits(ids, slots):
        member = jnp.where(hit, 1.0, member)
    before = lax.broadcasted_iota(jnp.int32, (count, count), 0) < lax.broadcasted_iota(
        jnp.int32, (count, count), 1
    )
    rank = contract(member.astype(BF16), before.astype(F32).astype(BF16), (1, 0))
    chosen = (member > 0.0) & (rank == slot)
    onehot = jnp.where(chosen, 1.0, 0.0).astype(BF16)
    select[...] = onehot
    start = pl.multiple_of(lax.axis_index("replica") * 2 * narrow, 2 * narrow)
    picked[...] = contract(onehot, tokens[:, pl.ds(start, 2 * narrow)], (1, 0)).astype(BF16)
    spread_members(order, picked, send, False)
    for dest in range(owners):
        rows = slice(dest * SLOT, (dest + 1) * SLOT)
        send[dest, 2 * SLOT : 3 * SLOT, :] = picked[rows, :narrow]
        send[dest, 3 * SLOT :, :] = picked[rows, narrow:]
    for load in loads:
        load.wait()


def weigh(ids, gates, select, weight):
    gate = jnp.zeros(select.shape, F32)
    for choice, hit in enumerate(expert_hits(ids, select.shape[0])):
        gate = jnp.where(hit, gates[choice : choice + 1, :], gate)
    weight[...] = jnp.sum(jnp.where(select[...].astype(F32) > 0.0, gate, 0.0), axis=1, keepdims=True)


def quad_slices(rows):
    quarter = rows // 4
    mine = lax.axis_index("expert") % 2 * 2 + lax.axis_index("group")
    flip = mine % 2 * 2 - 1
    diagonal = 3 - mine
    expert = diagonal + flip
    group = mine - flip
    return [pl.ds(pl.multiple_of(q * quarter, quarter), quarter) for q in (mine, diagonal, group, expert)]


def student_in(own, other, gate, up, keep, diagonal, group, expert, rows, pre):
    owners, _, narrow = own.shape
    full = 2 * owners * SLOT
    replica = lax.axis_index("replica")
    for part, at in ((own, replica), (other, 1 - replica)):
        columns = pl.ds(pl.multiple_of(at * narrow, narrow), narrow)
        rows[:, columns] = part[:, : 2 * SLOT, :].reshape(full, narrow)
    pieces = quad_slices(full)
    for index, matrix in enumerate((gate, up)):
        pre[...] = contract(rows[...], matrix[0], (1, 1))
        keep[index] = pre[pieces[0], :]
        for piece, out in zip(pieces[1:], (diagonal, group, expert)):
            out[index] = pre[piece, :].astype(BF16)


def student_mid(keep, diagonal, group, expert, pre, hidden):
    gate, up = (
        keep[i] + diagonal[i].astype(F32) + group[i].astype(F32) + expert[i].astype(F32) for i in range(2)
    )
    hidden[...] = hidden_of(gate, up)
    pre[0] = gate.astype(BF16)
    pre[1] = up.astype(BF16)


def half_slices(rows):
    half = rows // 2
    group = lax.axis_index("group")
    return [pl.ds(pl.multiple_of(at * half, half), half) for at in (group, 1 - group)]


def teacher_in(own, other, gate, up, keep, send, rows, pre):
    owners, _, narrow = own.shape
    replica = lax.axis_index("replica")
    for part, at in ((own, replica), (other, 1 - replica)):
        for piece in range(2):
            start = pl.multiple_of((2 * at + piece) * narrow, narrow)
            block = part[:, (2 + piece) * SLOT : (3 + piece) * SLOT, :]
            rows[:, pl.ds(start, narrow)] = block.reshape(owners * SLOT, narrow)
    mine, theirs = half_slices(pre.shape[0])
    for index, matrix in enumerate((gate, up)):
        pre[...] = contract(rows[...], matrix[0], (1, 1))
        keep[index] = pre[mine, :]
        send[index] = pre[theirs, :].astype(BF16)


def teacher_mid(keep, got, hidden):
    gate, up = (keep[i] + got[i].astype(F32) for i in range(2))
    hidden[...] = hidden_of(gate, up)


def hidden_of(gate, up):
    return (gate * jax.nn.sigmoid(gate) * up).astype(BF16)


def divide(hidden, down, keep, send):
    width = keep.shape[1]
    replica = lax.axis_index("replica")
    mine = pl.ds(pl.multiple_of(replica * width, width), width)
    theirs = pl.ds(pl.multiple_of((1 - replica) * width, width), width)
    send[...] = contract(hidden, down[0, :, theirs], (1, 0)).astype(BF16)
    keep[...] = contract(hidden, down[0, :, mine], (1, 0))


def student_out(own, diagonal, group, expert, down, keep, send, hidden):
    pieces = quad_slices(hidden.shape[0])
    for piece, part in zip(pieces, (own, diagonal, group, expert)):
        hidden[piece, :] = part[...]
    divide(hidden[...], down, keep, send)


def teacher_out(own, got, down, keep, send, hidden):
    for piece, part in zip(half_slices(hidden.shape[0]), (own, got)):
        hidden[piece, :] = part[...]
    divide(hidden[...], down, keep, send)


def join(stud, stud_got, teach, teach_got, send):
    owners, _, narrow = send.shape
    total = (stud[...] + stud_got[...].astype(F32)).astype(BF16)
    send[:, : 2 * SLOT, :] = total.reshape(owners, 2 * SLOT, narrow)
    total = (teach[...] + teach_got[...].astype(F32)).astype(BF16)
    for piece in range(2):
        block = total[:, piece * narrow : (piece + 1) * narrow].reshape(owners, SLOT, narrow)
        send[:, (2 + piece) * SLOT : (3 + piece) * SLOT, :] = block


def halves(value):
    high = value.astype(BF16)
    return high, (value - high.astype(F32)).astype(BF16)


def combine(order, back, select, weight, residual, send, stud, teach):
    owners, _, narrow = back.shape
    spread_members(order, back, stud, True)
    for dest in range(owners):
        rows = slice(dest * SLOT, (dest + 1) * SLOT)
        teach[rows, :narrow] = back[dest, 2 * SLOT : 3 * SLOT, :]
        teach[rows, narrow:] = back[dest, 3 * SLOT :, :]
    scale = weight[...]
    high, low = halves(scale * (stud[...].astype(F32) - teach[...].astype(F32)))
    onehot = select[...]
    total = contract(onehot, high, (0, 0)) + contract(onehot, low, (0, 0))
    residual[...] = total
    high, low = halves(total)
    rows = contract(onehot, high, (1, 0)) + contract(onehot, low, (1, 0))
    stud[...] = (scale * rows).astype(BF16)
    spread_members(order, stud, send, False)


def hidden_back(own, other, down, first, second, rows):
    owners, _, narrow = own.shape
    half = owners * SLOT
    replica = lax.axis_index("replica")
    for part, at in ((own, replica), (other, 1 - replica)):
        columns = pl.ds(pl.multiple_of(at * narrow, narrow), narrow)
        rows[:, columns] = part[...].reshape(2 * half, narrow)
    back = contract(rows[...], down[0], (1, 1)).astype(BF16)
    first[...] = back[:half]
    second[...] = back[half:]


def down_grad(hidden, rows, out):
    out[0] = contract(hidden[...], rows[...], (0, 0)).astype(BF16)


def slopes(own, diagonal, group, expert, out):
    pieces = quad_slices(out.shape[1])
    for piece, part in zip(pieces, (own, diagonal, group, expert)):
        gate, up = part[0].astype(F32), part[1].astype(F32)
        sig = jax.nn.sigmoid(gate)
        out[0, piece, :] = up * sig * (1.0 + gate * (1.0 - sig))
        out[1, piece, :] = gate * sig


def grads(slope, a_own, a_got, b_own, b_got, rows, gate_out, up_out, left):
    half = a_own.shape[0]
    for at, (own, got) in enumerate(((a_own, a_got), (b_own, b_got))):
        back = own[...].astype(F32) + got[...].astype(F32)
        block = slice(at * half, (at + 1) * half)
        for index in range(2):
            left[index, block, :] = (back * slope[index, block, :]).astype(BF16)
    gate_out[0] = contract(left[0], rows[...], (0, 0)).astype(BF16)
    up_out[0] = contract(left[1], rows[...], (0, 0)).astype(BF16)


def sum_bf16(own, got):
    return (own.astype(F32) + got.astype(F32)).astype(BF16)


def shards(tokens, expert_ids, route_gates, member_order, teach_gate, teach_up, teach_down, stud_gate, stud_up, stud_down):
    owners = lax.axis_size("expert")
    count, half_width = tokens.shape
    _, units, width = stud_gate.shape
    block = half_width // 2
    narrow = width // 2
    slots = owners * SLOT
    full = 2 * slots
    send, select, gate_near, up_near = call(
        route,
        [
            struct(BF16, owners, 4 * SLOT, narrow),
            struct(BF16, slots, count),
            struct(BF16, 1, units, width),
            struct(BF16, 1, units, width),
        ],
        [member_order, stud_gate, stud_up, expert_ids.T, tokens],
        [pltpu.VMEM((slots, block), BF16), pltpu.SemaphoreType.DMA((2,))],
        smem=1,
        far=2,
        flops=2 * slots * count * block,
        space=pltpu.HBM,
    )
    (weight,) = call(weigh, [struct(F32, slots, 1)], [expert_ids.T, route_gates.T, select])
    own = exchange(send)
    other = swap(own, "replica")
    quarter = full // 4
    pieces = [struct(BF16, 2, quarter, units)] * 3
    keep, *parts, stud_rows = call(
        student_in,
        [struct(F32, 2, quarter, units), *pieces, struct(BF16, full, width)],
        [own, other, gate_near, up_near],
        [pltpu.VMEM((full, units), F32)],
        flops=4 * full * width * units,
    )
    parts = quad(*parts)
    half = slots // 2
    teach_keep, teach_send = call(
        teacher_in,
        [struct(F32, 2, half, units), struct(BF16, 2, half, units)],
        [own, other, teach_gate, teach_up],
        [pltpu.VMEM((slots, half_width), BF16), pltpu.VMEM((slots, units), F32)],
        flops=4 * slots * half_width * units,
    )
    teach_got = swap(teach_send, "group")
    (teach_hidden,) = call(teacher_mid, [struct(BF16, half, units)], [teach_keep, teach_got])
    teach_got = swap(teach_hidden, "group")
    pre, hidden_piece = call(
        student_mid,
        [struct(BF16, 2, quarter, units), struct(BF16, quarter, units)],
        [keep, *parts],
    )
    hidden_parts = (hidden_piece, *quad(*[hidden_piece] * 3))
    pre_parts = (pre, *quad(*[pre] * 3))
    teach_keep, teach_send = call(
        teacher_out,
        [struct(F32, slots, block), struct(BF16, slots, block)],
        [teach_hidden, teach_got, teach_down],
        [pltpu.VMEM((slots, units), BF16)],
        flops=2 * slots * half_width * units,
    )
    teach_swap = swap(teach_send, "replica")
    stud_keep, stud_send, hidden = call(
        student_out,
        [struct(F32, full, narrow), struct(BF16, full, narrow), struct(BF16, full, units)],
        [*hidden_parts, stud_down],
        flops=2 * full * width * units,
    )
    stud_swap = swap(stud_send, "replica")
    (returned,) = call(
        join,
        [struct(BF16, owners, 4 * SLOT, narrow)],
        [stud_keep, stud_swap, teach_keep, teach_swap],
    )
    back = exchange(returned)
    residual, grad_send = call(
        combine,
        [struct(F32, count, block), struct(BF16, owners, 2 * SLOT, narrow)],
        [member_order, back, select, weight],
        [pltpu.VMEM((slots, block), BF16), pltpu.VMEM((slots, block), BF16)],
        smem=1,
        flops=8 * slots * count * block,
    )
    grad_own = exchange(grad_send)
    grad_other = swap(grad_own, "replica")
    back_first, back_second, grad_rows = call(
        hidden_back,
        [struct(BF16, slots, units), struct(BF16, slots, units), struct(BF16, full, width)],
        [grad_own, grad_other, stud_down],
        flops=2 * full * width * units,
    )
    back_first_one = swap(back_first, "group")
    back_second_one = swap(back_second, "expert")
    (grad_down,) = call(
        down_grad,
        [result(BF16, 1, units, width)],
        [hidden, grad_rows],
        flops=2 * full * width * units,
    )
    back_first = sum_bf16(back_first, back_first_one)
    back_second = sum_bf16(back_second, back_second_one)
    back_first_two = swap(back_first, "expert")
    back_second_two = swap(back_second, "group")
    (slope,) = call(slopes, [struct(F32, 2, full, units)], [*pre_parts])
    grad_gate, grad_up = call(
        grads,
        [result(BF16, 1, units, width), result(BF16, 1, units, width)],
        [slope, back_first, back_first_two, back_second, back_second_two, stud_rows],
        [pltpu.VMEM((2, full, units), BF16)],
        flops=4 * full * width * units,
    )
    return (residual, grad_gate, grad_up, grad_down)


def solution(mesh):
    weights = P("expert", "replica", "group")
    placed = (P("expert", "group"), P("expert", None), P("expert", None), P()) + (weights,) * 6
    return jax.shard_map(
        shards,
        mesh=mesh,
        in_specs=placed,
        out_specs=(P("expert", ("group", "replica")), weights, weights, weights),
        check_vma=False,
    )
```

profile of v0, /device:TPU:0, one launch (start us, length us, event | category | flops | bytes accessed | tf_op | source)
XLA Modules:
  0.0 118.7 jit_solution(875907574099420607)
XLA Ops:
  0.6 0.0 copy-start.1
  0.6 3.2 %shard_map.129 = (bf16[8,64,512]{2,1,0:T(8,128)(2,1)S(1)}, bf16[128,192]{1,0:T(8,128)(2,1)S(1)}, bf16[1,768,1024]{2,1,0:T(8,128)(2,1)S(1)}, bf16[1,768,1024]{2,1,0:T(8,128)(2,1)S(1)}) custom-call(s32[8]{0:T(128)} %order.3, bf16[1,768,1024]{2,1,0:T(8,128)(2,1)} %gate_hbm.1, bf16[1,768,1024]{2,1,0:T(8,128)(2,1)} %up_hbm.1, s32[8,192]{1,0:T(8,128)} %bitcast.2, ...), custom_call_target="tpu_custom_call" | custom-call | flops 50331648 | bytes 3938336 | tf_op jit(solution)/shard_map/pallas_call | solution.py:43
  3.9 21.6 %all_to_all.15.own = bf16[8,64,512]{2,1,0:T(8,128)(2,1)S(1)} all-to-all(bf16[8,64,512]{2,1,0:T(8,128)(2,1)S(1)} %get-tuple-element.29), channel_id=1, replica_groups=mesh['expert'=8,'replica'=2,'group'=2] {'expert'}, dimensions={0} | all-to-all | bytes 1048576 | tf_op jit(solution)/shard_map/all_to_all | solution.py:29
  25.5 0.0 collective-permute-start
  25.5 1.9 %collective-permute-done.other = bf16[8,64,512]{2,1,0:T(8,128)(2,1)S(1)} collective-permute-done((bf16[8,64,512]{2,1,0:T(8,128)(2,1)S(1)}, bf16[8,64,512]{2,1,0:T(8,128)(2,1)S(1)}, u32[]{:S(2)}, u32[]{:S(2)}) %collective-permute-start) | collective-permute-done | bytes 524320 | tf_op jit(solution)/shard_map/ppermute | solution.py:18
  27.4 0.0 copy-done.1
  27.4 1.9 %copy-done.2 = bf16[1,768,2048]{2,1,0:T(8,128)(2,1)S(1)} copy-done((bf16[1,768,2048]{2,1,0:T(8,128)(2,1)S(1)}, bf16[1,768,2048]{2,1,0:T(8,128)(2,1)}, u32[]{:S(2)}) %copy-start.2) | copy-done | bytes 3145752
  29.3 2.3 %shard_map.133 = (f32[2,64,768]{2,1,0:T(8,128)S(1)}, bf16[2,64,768]{2,1,0:T(8,128)(2,1)S(1)}) custom-call(bf16[8,64,512]{2,1,0:T(8,128)(2,1)S(1)} %all_to_all.15.own, bf16[8,64,512]{2,1,0:T(8,128)(2,1)S(1)} %collective-permute-done.other, bf16[1,768,2048]{2,1,0:T(8,128)(2,1)S(1)} %copy-done.1, bf16[1,768,2048]{2,1,0:T(8,128)(2,1)S(1)} %copy-done.2), custom_call_target="tpu_custom_call" | custom-call | flops 805306368 | bytes 7340032 | tf_op jit(solution)/shard_map/pallas_call | solution.py:43
  31.6 1.6 %collective-permute-start.8 = (bf16[2,64,768]{2,1,0:T(8,128)(2,1)S(1)}, bf16[2,64,768]{2,1,0:T(8,128)(2,1)S(1)}, u32[]{:S(2)}, u32[]{:S(2)}) collective-permute-start(bf16[2,64,768]{2,1,0:T(8,128)(2,1)S(1)} %get-tuple-element.40), channel_id=1, source_target_pairs={{0,1},{1,0},{2,3},{3,2},{4,5},{5,4},{6,7},{7,6},{8,9},{9,8},{10,11... | collective-permute-start | bytes 589832 | tf_op jit(solution)/shard_map/ppermute | solution.py:18
  33.2 1.1 shard_map.130
  34.3 1.4 %collective-permute-start.1 = (bf16[2,64,768]{2,1,0:T(8,128)(2,1)S(1)}, bf16[2,64,768]{2,1,0:T(8,128)(2,1)S(1)}, u32[]{:S(2)}, u32[]{:S(2)}) collective-permute-start(bf16[2,64,768]{2,1,0:T(8,128)(2,1)S(1)} %get-tuple-element.33), channel_id=1, source_target_pairs={{0,5},{1,4},{4,1},{5,0},{8,13},{9,12},{12,9},{13,8},{16,21},{17,20... | collective-permute-start | bytes 589832 | tf_op jit(solution)/shard_map/ppermute | solution.py:24
  35.7 1.5 %collective-permute-start.2 = (bf16[2,64,768]{2,1,0:T(8,128)(2,1)S(1)}, bf16[2,64,768]{2,1,0:T(8,128)(2,1)S(1)}, u32[]{:S(2)}, u32[]{:S(2)}) collective-permute-start(bf16[2,64,768]{2,1,0:T(8,128)(2,1)S(1)} %get-tuple-element.34), channel_id=1, source_target_pairs={{0,1},{1,0},{2,3},{3,2},{4,5},{5,4},{6,7},{7,6},{8,9},{9,8},{10,11... | collective-permute-start | bytes 589832 | tf_op jit(solution)/shard_map/ppermute | solution.py:18
  37.2 0.6 collective-permute-start.3
  37.8 1.6 %collective-permute-done.8.got = bf16[2,64,768]{2,1,0:T(8,128)(2,1)S(1)} collective-permute-done((bf16[2,64,768]{2,1,0:T(8,128)(2,1)S(1)}, bf16[2,64,768]{2,1,0:T(8,128)(2,1)S(1)}, u32[]{:S(2)}, u32[]{:S(2)}) %collective-permute-start.8) | collective-permute-done | bytes 196640 | tf_op jit(solution)/shard_map/ppermute | solution.py:18
  39.4 0.1 shard_map.134.own
  39.5 1.6 %collective-permute-start.9 = (bf16[64,768]{1,0:T(8,128)(2,1)S(1)}, bf16[64,768]{1,0:T(8,128)(2,1)S(1)}, u32[]{:S(2)}, u32[]{:S(2)}) collective-permute-start(bf16[64,768]{1,0:T(8,128)(2,1)S(1)} %shard_map.134.own), channel_id=1, source_target_pairs={{0,1},{1,0},{2,3},{3,2},{4,5},{5,4},{6,7},{7,6},{8,9},{9,8},{10,11... | collective-permute-start | bytes 294920 | tf_op jit(solution)/shard_map/ppermute | solution.py:18
  41.1 3.5 %collective-permute-done.1.diagonal = bf16[2,64,768]{2,1,0:T(8,128)(2,1)S(1)} collective-permute-done((bf16[2,64,768]{2,1,0:T(8,128)(2,1)S(1)}, bf16[2,64,768]{2,1,0:T(8,128)(2,1)S(1)}, u32[]{:S(2)}, u32[]{:S(2)}) %collective-permute-start.1) | collective-permute-done | bytes 196640 | tf_op jit(solution)/shard_map/ppermute | solution.py:24
  44.6 3.3 %collective-permute-done.2.group = bf16[2,64,768]{2,1,0:T(8,128)(2,1)S(1)} collective-permute-done((bf16[2,64,768]{2,1,0:T(8,128)(2,1)S(1)}, bf16[2,64,768]{2,1,0:T(8,128)(2,1)S(1)}, u32[]{:S(2)}, u32[]{:S(2)}) %collective-permute-start.2) | collective-permute-done | bytes 196640 | tf_op jit(solution)/shard_map/ppermute | solution.py:18
  47.9 0.0 collective-permute-done.3.expert
  47.9 0.1 shard_map.131
  48.0 0.0 copy-start
  48.1 1.5 %collective-permute-start.6 = (bf16[64,768]{1,0:T(8,128)(2,1)S(1)}, bf16[64,768]{1,0:T(8,128)(2,1)S(1)}, u32[]{:S(2)}, u32[]{:S(2)}) collective-permute-start(bf16[64,768]{1,0:T(8,128)(2,1)S(1)} %get-tuple-element.36.own), channel_id=1, source_target_pairs={{0,4},{4,0},{8,12},{12,8},{16,20},{20,16},{24,28},{28,24},{1,5},{5... | collective-permute-start | bytes 294920 | tf_op jit(solution)/shard_map/ppermute | solution.py:18
  49.5 1.5 %collective-permute-start.5 = (bf16[64,768]{1,0:T(8,128)(2,1)S(1)}, bf16[64,768]{1,0:T(8,128)(2,1)S(1)}, u32[]{:S(2)}, u32[]{:S(2)}) collective-permute-start(bf16[64,768]{1,0:T(8,128)(2,1)S(1)} %get-tuple-element.36.own), channel_id=1, source_target_pairs={{0,1},{1,0},{2,3},{3,2},{4,5},{5,4},{6,7},{7,6},{8,9},{9,8},{10,11... | collective-permute-start | bytes 294920 | tf_op jit(solution)/shard_map/ppermute | solution.py:18
  51.0 0.6 collective-permute-start.4
  51.6 0.0 collective-permute-done.9.got
  51.6 0.0 copy-done.3
  51.6 0.6 shard_map.135
  52.2 0.1 collective-permute-start.10
  52.3 1.5 %collective-permute-done.6.expert = bf16[64,768]{1,0:T(8,128)(2,1)S(1)} collective-permute-done((bf16[64,768]{1,0:T(8,128)(2,1)S(1)}, bf16[64,768]{1,0:T(8,128)(2,1)S(1)}, u32[]{:S(2)}, u32[]{:S(2)}) %collective-permute-start.6) | collective-permute-done | bytes 98336 | tf_op jit(solution)/shard_map/ppermute | solution.py:18
  53.8 0.4 collective-permute-done.5.group
  54.2 2.4 %collective-permute-done.4.diagonal = bf16[64,768]{1,0:T(8,128)(2,1)S(1)} collective-permute-done((bf16[64,768]{1,0:T(8,128)(2,1)S(1)}, bf16[64,768]{1,0:T(8,128)(2,1)S(1)}, u32[]{:S(2)}, u32[]{:S(2)}) %collective-permute-start.4) | collective-permute-done | bytes 98336 | tf_op jit(solution)/shard_map/ppermute | solution.py:24
  56.6 0.6 shard_map.132
  57.2 0.1 collective-permute-start.7
  57.2 0.0 collective-permute-done.10.teach_got
  57.3 1.5 %collective-permute-done.7.stud_got = bf16[256,512]{1,0:T(8,128)(2,1)S(1)} collective-permute-done((bf16[256,512]{1,0:T(8,128)(2,1)S(1)}, bf16[256,512]{1,0:T(8,128)(2,1)S(1)}, u32[]{:S(2)}, u32[]{:S(2)}) %collective-permute-start.7) | collective-permute-done | bytes 262176 | tf_op jit(solution)/shard_map/ppermute | solution.py:18
  58.8 0.9 shard_map.136
  59.6 3.5 %all-to-all-start.1 = ((bf16[8,64,512]{2,1,0:T(8,128)(2,1)}), bf16[8,64,512]{2,1,0:T(8,128)(2,1)S(1)}, u32[]{:S(2)}, u32[]{:S(2)}) async-start(bf16[8,64,512]{2,1,0:T(8,128)(2,1)} %shard_map.136), calls=%async_computation.1 | async-start | bytes 1048576 | tf_op jit(solution)/shard_map/all_to_all | solution.py:29
  63.2 0.0 copy-done.4
  63.2 0.0 copy-done.5
  63.2 0.2 shard_map.137.weight
  63.3 14.8 %all-to-all-done.1.back = bf16[8,64,512]{2,1,0:T(8,128)(2,1)S(1)} async-done(((bf16[8,64,512]{2,1,0:T(8,128)(2,1)}), bf16[8,64,512]{2,1,0:T(8,128)(2,1)S(1)}, u32[]{:S(2)}, u32[]{:S(2)}) %all-to-all-start.1) | async-done | bytes 524320 | tf_op jit(solution)/shard_map/all_to_all | solution.py:29
  78.1 1.4 %shard_map.138 = (f32[192,1024]{1,0:T(8,128)S(1)}, bf16[8,32,512]{2,1,0:T(8,128)(2,1)S(1)}) custom-call(s32[8]{0:T(128)} %order.3, bf16[8,64,512]{2,1,0:T(8,128)(2,1)S(1)} %all-to-all-done.1.back, bf16[128,192]{1,0:T(8,128)(2,1)S(1)} %get-tuple-element.43.select, f32[128,1]{1,0:T(8,128)S(1)} %shard_map.137.weight), custom_call_target="tpu_custom_call" | custom-call | flops 201326592 | bytes 573984 | tf_op jit(solution)/shard_map/pallas_call | solution.py:43
  79.5 12.5 %all_to_all.16.own = bf16[8,32,512]{2,1,0:T(8,128)(2,1)S(1)} all-to-all(bf16[8,32,512]{2,1,0:T(8,128)(2,1)S(1)} %get-tuple-element.46), channel_id=1, replica_groups=mesh['expert'=8,'replica'=2,'group'=2] {'expert'}, dimensions={0} | all-to-all | bytes 524288 | tf_op jit(solution)/shard_map/all_to_all | solution.py:29
  92.1 0.0 collective-permute-start.14
  92.1 1.5 %collective-permute-done.14.other = bf16[8,32,512]{2,1,0:T(8,128)(2,1)S(1)} collective-permute-done((bf16[8,32,512]{2,1,0:T(8,128)(2,1)S(1)}, bf16[8,32,512]{2,1,0:T(8,128)(2,1)S(1)}, u32[]{:S(2)}, u32[]{:S(2)}) %collective-permute-start.14) | collective-permute-done | bytes 262176 | tf_op jit(solution)/shard_map/ppermute | solution.py:18
  93.6 0.6 shard_map.140
  94.2 0.6 collective-permute-start.15
  94.8 1.4 %collective-permute-start.13 = (bf16[2,64,768]{2,1,0:T(8,128)(2,1)S(1)}, bf16[2,64,768]{2,1,0:T(8,128)(2,1)S(1)}, u32[]{:S(2)}, u32[]{:S(2)}) collective-permute-start(bf16[2,64,768]{2,1,0:T(8,128)(2,1)S(1)} %get-tuple-element.45.own), channel_id=1, source_target_pairs={{0,4},{4,0},{8,12},{12,8},{16,20},{20,16},{24,28},{28,24},{1,5},{5... | collective-permute-start | bytes 589832 | tf_op jit(solution)/shard_map/ppermute | solution.py:18
  96.2 1.5 %collective-permute-start.12 = (bf16[2,64,768]{2,1,0:T(8,128)(2,1)S(1)}, bf16[2,64,768]{2,1,0:T(8,128)(2,1)S(1)}, u32[]{:S(2)}, u32[]{:S(2)}) collective-permute-start(bf16[2,64,768]{2,1,0:T(8,128)(2,1)S(1)} %get-tuple-element.45.own), channel_id=1, source_target_pairs={{0,1},{1,0},{2,3},{3,2},{4,5},{5,4},{6,7},{7,6},{8,9},{9,8},{10,11... | collective-permute-start | bytes 589832 | tf_op jit(solution)/shard_map/ppermute | solution.py:18
  97.7 0.6 collective-permute-start.11
  98.3 1.4 %collective-permute-start.17 = (bf16[128,768]{1,0:T(8,128)(2,1)S(1)}, bf16[128,768]{1,0:T(8,128)(2,1)S(1)}, u32[]{:S(2)}, u32[]{:S(2)}) collective-permute-start(bf16[128,768]{1,0:T(8,128)(2,1)S(1)} %get-tuple-element.48), channel_id=1, source_target_pairs={{0,4},{4,0},{8,12},{12,8},{16,20},{20,16},{24,28},{28,24},{1,5},{5... | collective-permute-start | bytes 589832 | tf_op jit(solution)/shard_map/ppermute | solution.py:18
  99.7 2.3 %collective-permute-done.15 = bf16[128,768]{1,0:T(8,128)(2,1)S(1)} collective-permute-done((bf16[128,768]{1,0:T(8,128)(2,1)S(1)}, bf16[128,768]{1,0:T(8,128)(2,1)S(1)}, u32[]{:S(2)}, u32[]{:S(2)}) %collective-permute-start.15) | collective-permute-done | bytes 196640 | tf_op jit(solution)/shard_map/ppermute | solution.py:18
  102.1 1.5 %collective-permute-start.16 = (bf16[128,768]{1,0:T(8,128)(2,1)S(1)}, bf16[128,768]{1,0:T(8,128)(2,1)S(1)}, u32[]{:S(2)}, u32[]{:S(2)}) collective-permute-start(bf16[128,768]{1,0:T(8,128)(2,1)S(1)} %add_convert_fusion.1.a_own), channel_id=1, source_target_pairs={{0,4},{4,0},{8,12},{12,8},{16,20},{20,16},{24,28},{28,24},{1,5},{5... | collective-permute-start | bytes 589832 | tf_op jit(solution)/shard_map/ppermute | solution.py:18
  103.6 7.1 %collective-permute-done.17 = bf16[128,768]{1,0:T(8,128)(2,1)S(1)} collective-permute-done((bf16[128,768]{1,0:T(8,128)(2,1)S(1)}, bf16[128,768]{1,0:T(8,128)(2,1)S(1)}, u32[]{:S(2)}, u32[]{:S(2)}) %collective-permute-start.17) | collective-permute-done | bytes 196640 | tf_op jit(solution)/shard_map/ppermute | solution.py:18
  110.7 1.9 %collective-permute-start.18 = (bf16[128,768]{1,0:T(8,128)(2,1)S(1)}, bf16[128,768]{1,0:T(8,128)(2,1)S(1)}, u32[]{:S(2)}, u32[]{:S(2)}) collective-permute-start(bf16[128,768]{1,0:T(8,128)(2,1)S(1)} %add_convert_fusion.b_own), channel_id=1, source_target_pairs={{0,1},{1,0},{2,3},{3,2},{4,5},{5,4},{6,7},{7,6},{8,9},{9,8},{10,11... | collective-permute-start | bytes 589832 | tf_op jit(solution)/shard_map/ppermute | solution.py:18
  112.6 0.0 collective-permute-done.13.expert
  112.6 0.0 collective-permute-done.12.group
  112.6 0.0 collective-permute-done.11.diagonal
  112.6 0.3 shard_map.139.slope
  113.0 0.9 copy.14
  113.8 1.7 %shard_map.142 = bf16[1,768,1024]{2,1,0:T(8,128)(2,1)} custom-call(bf16[256,768]{1,0:T(8,128)(2,1)S(1)} %get-tuple-element.52.hidden, bf16[256,1024]{1,0:T(8,128)(2,1)S(1)} %get-tuple-element.53.rows), custom_call_target="tpu_custom_call" | custom-call | flops 402653184 | bytes 917504 | tf_op jit(solution)/shard_map/pallas_call | solution.py:43
  115.6 0.0 collective-permute-done.16.a_got
  115.6 0.9 collective-permute-done.18.b_got
  116.4 2.3 %shard_map.141 = (bf16[1,768,1024]{2,1,0:T(8,128)(2,1)}, bf16[1,768,1024]{2,1,0:T(8,128)(2,1)}) custom-call(f32[2,256,768]{2,1,0:T(8,128)S(1)} %shard_map.139.slope, bf16[128,768]{1,0:T(8,128)(2,1)S(1)} %add_convert_fusion.1.a_own, bf16[128,768]{1,0:T(8,128)(2,1)S(1)} %collective-permute-done.16.a_got, bf16[128,768]{1,0:T(8,128)(2,1)S(1)} %add_convert_fusion.b_own, ...), custom_call_target="tpu_custom_call" | custom-call | flops 805306368 | bytes 2883584 | tf_op jit(solution)/shard_map/pallas_call | solution.py:43
  (7 shorter events, 0.1 us)
Async XLA Ops:
  0.6 26.8 %copy-start.1 = (bf16[1,768,2048]{2,1,0:T(8,128)(2,1)S(1)}, bf16[1,768,2048]{2,1,0:T(8,128)(2,1)}, u32[]{:S(2)}) copy-start(bf16[1,768,2048]{2,1,0:T(8,128)(2,1)} %gate.1) | copy-start | bytes 9437188
  25.5 1.9 %collective-permute-start = (bf16[8,64,512]{2,1,0:T(8,128)(2,1)S(1)}, bf16[8,64,512]{2,1,0:T(8,128)(2,1)S(1)}, u32[]{:S(2)}, u32[]{:S(2)}) collective-permute-start(bf16[8,64,512]{2,1,0:T(8,128)(2,1)S(1)} %all_to_all.15.own), channel_id=1, source_target_pairs={{0,2},{2,0},{1,3},{3,1},{4,6},{6,4},{5,7},{7,5},{8,10},{10,8},{9,1... | collective-permute-start | bytes 1572872 | tf_op jit(solution)/shard_map/ppermute | solution.py:18
  27.4 1.9 %copy-start.2 = (bf16[1,768,2048]{2,1,0:T(8,128)(2,1)S(1)}, bf16[1,768,2048]{2,1,0:T(8,128)(2,1)}, u32[]{:S(2)}) copy-start(bf16[1,768,2048]{2,1,0:T(8,128)(2,1)} %up.1) | copy-start | bytes 9437188
  31.6 7.8 %collective-permute-start.8 = (bf16[2,64,768]{2,1,0:T(8,128)(2,1)S(1)}, bf16[2,64,768]{2,1,0:T(8,128)(2,1)S(1)}, u32[]{:S(2)}, u32[]{:S(2)}) collective-permute-start(bf16[2,64,768]{2,1,0:T(8,128)(2,1)S(1)} %get-tuple-element.40), channel_id=1, source_target_pairs={{0,1},{1,0},{2,3},{3,2},{4,5},{5,4},{6,7},{7,6},{8,9},{9,8},{10,11... | collective-permute-start | bytes 589832 | tf_op jit(solution)/shard_map/ppermute | solution.py:18
  33.2 18.4 %copy-start.3 = (bf16[1,768,2048]{2,1,0:T(8,128)(2,1)S(1)}, bf16[1,768,2048]{2,1,0:T(8,128)(2,1)}, u32[]{:S(2)}) copy-start(bf16[1,768,2048]{2,1,0:T(8,128)(2,1)} %down.4) | copy-start | bytes 9437188
  34.3 10.3 %collective-permute-start.1 = (bf16[2,64,768]{2,1,0:T(8,128)(2,1)S(1)}, bf16[2,64,768]{2,1,0:T(8,128)(2,1)S(1)}, u32[]{:S(2)}, u32[]{:S(2)}) collective-permute-start(bf16[2,64,768]{2,1,0:T(8,128)(2,1)S(1)} %get-tuple-element.33), channel_id=1, source_target_pairs={{0,5},{1,4},{4,1},{5,0},{8,13},{9,12},{12,9},{13,8},{16,21},{17,20... | collective-permute-start | bytes 589832 | tf_op jit(solution)/shard_map/ppermute | solution.py:24
  35.7 12.2 %collective-permute-start.2 = (bf16[2,64,768]{2,1,0:T(8,128)(2,1)S(1)}, bf16[2,64,768]{2,1,0:T(8,128)(2,1)S(1)}, u32[]{:S(2)}, u32[]{:S(2)}) collective-permute-start(bf16[2,64,768]{2,1,0:T(8,128)(2,1)S(1)} %get-tuple-element.34), channel_id=1, source_target_pairs={{0,1},{1,0},{2,3},{3,2},{4,5},{5,4},{6,7},{7,6},{8,9},{9,8},{10,11... | collective-permute-start | bytes 589832 | tf_op jit(solution)/shard_map/ppermute | solution.py:18
  37.2 10.7 %collective-permute-start.3 = (bf16[2,64,768]{2,1,0:T(8,128)(2,1)S(1)}, bf16[2,64,768]{2,1,0:T(8,128)(2,1)S(1)}, u32[]{:S(2)}, u32[]{:S(2)}) collective-permute-start(bf16[2,64,768]{2,1,0:T(8,128)(2,1)S(1)} %get-tuple-element.35), channel_id=1, source_target_pairs={{0,4},{4,0},{8,12},{12,8},{16,20},{20,16},{24,28},{28,24},{1,5},{5... | collective-permute-start | bytes 589832 | tf_op jit(solution)/shard_map/ppermute | solution.py:18
  39.5 12.1 %collective-permute-start.9 = (bf16[64,768]{1,0:T(8,128)(2,1)S(1)}, bf16[64,768]{1,0:T(8,128)(2,1)S(1)}, u32[]{:S(2)}, u32[]{:S(2)}) collective-permute-start(bf16[64,768]{1,0:T(8,128)(2,1)S(1)} %shard_map.134.own), channel_id=1, source_target_pairs={{0,1},{1,0},{2,3},{3,2},{4,5},{5,4},{6,7},{7,6},{8,9},{9,8},{10,11... | collective-permute-start | bytes 294920 | tf_op jit(solution)/shard_map/ppermute | solution.py:18
  48.0 8.5 %copy-start = (bf16[1,768,1024]{2,1,0:T(8,128)(2,1)S(1)}, bf16[1,768,1024]{2,1,0:T(8,128)(2,1)}, u32[]{:S(2)}) copy-start(bf16[1,768,1024]{2,1,0:T(8,128)(2,1)} %down.5) | copy-start | bytes 4718596
  48.1 5.7 %collective-permute-start.6 = (bf16[64,768]{1,0:T(8,128)(2,1)S(1)}, bf16[64,768]{1,0:T(8,128)(2,1)S(1)}, u32[]{:S(2)}, u32[]{:S(2)}) collective-permute-start(bf16[64,768]{1,0:T(8,128)(2,1)S(1)} %get-tuple-element.36.own), channel_id=1, source_target_pairs={{0,4},{4,0},{8,12},{12,8},{16,20},{20,16},{24,28},{28,24},{1,5},{5... | collective-permute-start | bytes 294920 | tf_op jit(solution)/shard_map/ppermute | solution.py:18
  49.5 4.6 %collective-permute-start.5 = (bf16[64,768]{1,0:T(8,128)(2,1)S(1)}, bf16[64,768]{1,0:T(8,128)(2,1)S(1)}, u32[]{:S(2)}, u32[]{:S(2)}) collective-permute-start(bf16[64,768]{1,0:T(8,128)(2,1)S(1)} %get-tuple-element.36.own), channel_id=1, source_target_pairs={{0,1},{1,0},{2,3},{3,2},{4,5},{5,4},{6,7},{7,6},{8,9},{9,8},{10,11... | collective-permute-start | bytes 294920 | tf_op jit(solution)/shard_map/ppermute | solution.py:18
  51.0 5.5 %collective-permute-start.4 = (bf16[64,768]{1,0:T(8,128)(2,1)S(1)}, bf16[64,768]{1,0:T(8,128)(2,1)S(1)}, u32[]{:S(2)}, u32[]{:S(2)}) collective-permute-start(bf16[64,768]{1,0:T(8,128)(2,1)S(1)} %get-tuple-element.36.own), channel_id=1, source_target_pairs={{0,5},{1,4},{4,1},{5,0},{8,13},{9,12},{12,9},{13,8},{16,21},{17,20... | collective-permute-start | bytes 294920 | tf_op jit(solution)/shard_map/ppermute | solution.py:24
  52.2 5.0 %collective-permute-start.10 = (bf16[128,1024]{1,0:T(8,128)(2,1)S(1)}, bf16[128,1024]{1,0:T(8,128)(2,1)S(1)}, u32[]{:S(2)}, u32[]{:S(2)}) collective-permute-start(bf16[128,1024]{1,0:T(8,128)(2,1)S(1)} %get-tuple-element.42), channel_id=1, source_target_pairs={{0,2},{2,0},{1,3},{3,1},{4,6},{6,4},{5,7},{7,5},{8,10},{10,8},{9,1... | collective-permute-start | bytes 786440 | tf_op jit(solution)/shard_map/ppermute | solution.py:18
  57.2 1.6 %collective-permute-start.7 = (bf16[256,512]{1,0:T(8,128)(2,1)S(1)}, bf16[256,512]{1,0:T(8,128)(2,1)S(1)}, u32[]{:S(2)}, u32[]{:S(2)}) collective-permute-start(bf16[256,512]{1,0:T(8,128)(2,1)S(1)} %get-tuple-element.38), channel_id=1, source_target_pairs={{0,2},{2,0},{1,3},{3,1},{4,6},{6,4},{5,7},{7,5},{8,10},{10,8},{9,1... | collective-permute-start | bytes 786440 | tf_op jit(solution)/shard_map/ppermute | solution.py:18
  58.8 4.4 %copy-start.4 = (s32[192,8]{0,1:T(8,128)S(1)}, s32[192,8]{0,1:T(8,128)}, u32[]{:S(2)}) copy-start(s32[192,8]{0,1:T(8,128)} %param.11) | copy-start | bytes 18436
  58.8 4.4 %copy-start.5 = (f32[192,8]{0,1:T(8,128)S(1)}, f32[192,8]{0,1:T(8,128)}, u32[]{:S(2)}) copy-start(f32[192,8]{0,1:T(8,128)} %param.12) | copy-start | bytes 18436
  59.6 18.5 %all-to-all-start.1 = ((bf16[8,64,512]{2,1,0:T(8,128)(2,1)}), bf16[8,64,512]{2,1,0:T(8,128)(2,1)S(1)}, u32[]{:S(2)}, u32[]{:S(2)}) async-start(bf16[8,64,512]{2,1,0:T(8,128)(2,1)} %shard_map.136), calls=%async_computation.1 | async-start | bytes 1048576 | tf_op jit(solution)/shard_map/all_to_all | solution.py:29
  92.1 1.5 %collective-permute-start.14 = (bf16[8,32,512]{2,1,0:T(8,128)(2,1)S(1)}, bf16[8,32,512]{2,1,0:T(8,128)(2,1)S(1)}, u32[]{:S(2)}, u32[]{:S(2)}) collective-permute-start(bf16[8,32,512]{2,1,0:T(8,128)(2,1)S(1)} %all_to_all.16.own), channel_id=1, source_target_pairs={{0,2},{2,0},{1,3},{3,1},{4,6},{6,4},{5,7},{7,5},{8,10},{10,8},{9,1... | collective-permute-start | bytes 786440 | tf_op jit(solution)/shard_map/ppermute | solution.py:18
  94.2 7.8 %collective-permute-start.15 = (bf16[128,768]{1,0:T(8,128)(2,1)S(1)}, bf16[128,768]{1,0:T(8,128)(2,1)S(1)}, u32[]{:S(2)}, u32[]{:S(2)}) collective-permute-start(bf16[128,768]{1,0:T(8,128)(2,1)S(1)} %get-tuple-element.47), channel_id=1, source_target_pairs={{0,1},{1,0},{2,3},{3,2},{4,5},{5,4},{6,7},{7,6},{8,9},{9,8},{10,11... | collective-permute-start | bytes 589832 | tf_op jit(solution)/shard_map/ppermute | solution.py:18
  94.8 17.8 %collective-permute-start.13 = (bf16[2,64,768]{2,1,0:T(8,128)(2,1)S(1)}, bf16[2,64,768]{2,1,0:T(8,128)(2,1)S(1)}, u32[]{:S(2)}, u32[]{:S(2)}) collective-permute-start(bf16[2,64,768]{2,1,0:T(8,128)(2,1)S(1)} %get-tuple-element.45.own), channel_id=1, source_target_pairs={{0,4},{4,0},{8,12},{12,8},{16,20},{20,16},{24,28},{28,24},{1,5},{5... | collective-permute-start | bytes 589832 | tf_op jit(solution)/shard_map/ppermute | solution.py:18
  96.2 16.4 %collective-permute-start.12 = (bf16[2,64,768]{2,1,0:T(8,128)(2,1)S(1)}, bf16[2,64,768]{2,1,0:T(8,128)(2,1)S(1)}, u32[]{:S(2)}, u32[]{:S(2)}) collective-permute-start(bf16[2,64,768]{2,1,0:T(8,128)(2,1)S(1)} %get-tuple-element.45.own), channel_id=1, source_target_pairs={{0,1},{1,0},{2,3},{3,2},{4,5},{5,4},{6,7},{7,6},{8,9},{9,8},{10,11... | collective-permute-start | bytes 589832 | tf_op jit(solution)/shard_map/ppermute | solution.py:18
  97.7 14.9 %collective-permute-start.11 = (bf16[2,64,768]{2,1,0:T(8,128)(2,1)S(1)}, bf16[2,64,768]{2,1,0:T(8,128)(2,1)S(1)}, u32[]{:S(2)}, u32[]{:S(2)}) collective-permute-start(bf16[2,64,768]{2,1,0:T(8,128)(2,1)S(1)} %get-tuple-element.45.own), channel_id=1, source_target_pairs={{0,5},{1,4},{4,1},{5,0},{8,13},{9,12},{12,9},{13,8},{16,21},{17,20... | collective-permute-start | bytes 589832 | tf_op jit(solution)/shard_map/ppermute | solution.py:24
  98.3 12.3 %collective-permute-start.17 = (bf16[128,768]{1,0:T(8,128)(2,1)S(1)}, bf16[128,768]{1,0:T(8,128)(2,1)S(1)}, u32[]{:S(2)}, u32[]{:S(2)}) collective-permute-start(bf16[128,768]{1,0:T(8,128)(2,1)S(1)} %get-tuple-element.48), channel_id=1, source_target_pairs={{0,4},{4,0},{8,12},{12,8},{16,20},{20,16},{24,28},{28,24},{1,5},{5... | collective-permute-start | bytes 589832 | tf_op jit(solution)/shard_map/ppermute | solution.py:18
  102.1 13.5 %collective-permute-start.16 = (bf16[128,768]{1,0:T(8,128)(2,1)S(1)}, bf16[128,768]{1,0:T(8,128)(2,1)S(1)}, u32[]{:S(2)}, u32[]{:S(2)}) collective-permute-start(bf16[128,768]{1,0:T(8,128)(2,1)S(1)} %add_convert_fusion.1.a_own), channel_id=1, source_target_pairs={{0,4},{4,0},{8,12},{12,8},{16,20},{20,16},{24,28},{28,24},{1,5},{5... | collective-permute-start | bytes 589832 | tf_op jit(solution)/shard_map/ppermute | solution.py:18
  110.7 5.7 %collective-permute-start.18 = (bf16[128,768]{1,0:T(8,128)(2,1)S(1)}, bf16[128,768]{1,0:T(8,128)(2,1)S(1)}, u32[]{:S(2)}, u32[]{:S(2)}) collective-permute-start(bf16[128,768]{1,0:T(8,128)(2,1)S(1)} %add_convert_fusion.b_own), channel_id=1, source_target_pairs={{0,1},{1,0},{2,3},{3,2},{4,5},{5,4},{6,7},{7,6},{8,9},{9,8},{10,11... | collective-permute-start | bytes 589832 | tf_op jit(solution)/shard_map/ppermute | solution.py:18
where the time goes:
time: 119 us
  waiting for transfers between devices  42.7 us (36%)
  blocking collectives  34.2 us (29%)
  starting transfers between devices  22.8 us (19%)
  Pallas kernels  15.4 us (13%)
  local copies, waits for them, and re-layouts  2.79 us (2%)
    all_to_all x2, blocking collectives, exchange(): lax.all_to_all(block, 'expert', split_axis=0, concat_axis=0, tiled=True)  34.2 us
    ppermute x16, waiting for transfers between devices, swap(): lax.ppermute(block, axis, [(place, place ^ 1) for place in range(count)])  22 us
    ppermute x16, starting transfers between devices, swap(): lax.ppermute(block, axis, [(place, place ^ 1) for place in range(count)])  16.7 us
    pallas_call x14, Pallas kernels, call(): pl.pallas_call(body, out_shape=outs, in_specs=specs, out_specs=[pl.BlockS...  15.4 us
    all_to_all x1, waiting for transfers between devices, exchange(): lax.all_to_all(block, 'expert', split_axis=0, concat_axis=0, tiled=True)  14.8 us
    ppermute x3, waiting for transfers between devices, quad(): diagonal = lax.ppermute(diagonal, ('expert', 'group'), crossing)  5.88 us
    all_to_all x1, starting transfers between devices, exchange(): lax.all_to_all(block, 'expert', split_axis=0, concat_axis=0, tiled=True)  3.49 us
    unnamed x13, local copies, waits for them, and re-layouts  2.79 us
  transfers between devices with their start and end apart: 20, of which 13 were waited for; matrix products, arithmetic and copies ran while one was open for 1% of the time, Pallas kernels for 4%

commit v1 on v0

--- a/solution.py
+++ b/solution.py
@@ -7,6 +7,7 @@
 
 
 SLOT = 16
+TILE = 256
 
 
 BF16 = jnp.bfloat16
@@ -33,7 +34,7 @@
     return lax.dot_general(left, right, ((dims[:1], dims[1:]), ((), ())), preferred_element_type=F32)
 
 
-def call(body, outs, ins, scratch=(), smem=0, far=0, flops=0, limit=16, space=pltpu.VMEM):
+def call(body, outs, ins, scratch=(), smem=0, far=0, far_outs=0, flops=0, limit=16, space=pltpu.VMEM):
     specs = [pl.BlockSpec(memory_space=pltpu.SMEM)] * smem
     specs += [pl.BlockSpec(memory_space=pltpu.HBM)] * far
     specs += [pl.BlockSpec(memory_space=pltpu.VMEM)] * (len(ins) - smem - far)
@@ -44,7 +45,8 @@
         body,
         out_shape=outs,
         in_specs=specs,
-        out_specs=[pl.BlockSpec(memory_space=pltpu.VMEM)] * len(outs),
+        out_specs=[pl.BlockSpec(memory_space=pltpu.HBM)] * far_outs
+        + [pl.BlockSpec(memory_space=pltpu.VMEM)] * (len(outs) - far_outs),
         scratch_shapes=scratch,
         cost_estimate=pl.CostEstimate(flops=flops, bytes_accessed=moved, transcendentals=0),
         compiler_params=pltpu.CompilerParams(vmem_limit_bytes=limit << 20),
@@ -84,8 +86,9 @@
     return [ids[choice : choice + 1, :] == expert for choice in range(ids.shape[0])]
 
 
-def route(order, gate_hbm, up_hbm, ids, tokens, send, select, gate_near, up_near, picked, arrived):
-    loads = loads_of(arrived, (gate_hbm, gate_near), (up_hbm, up_near))
+def route(order, up_hbm, ids, tokens, send, select, up_near, picked, arrived):
+    load = pltpu.make_async_copy(up_hbm, up_near, arrived)
+    load.start()
     owners, _, narrow = send.shape
     slots, count = select.shape
     slot = (lax.broadcasted_iota(jnp.int32, (slots, count), 0) % SLOT).astype(F32)
@@ -106,8 +109,7 @@
         rows = slice(dest * SLOT, (dest + 1) * SLOT)
         send[dest, 2 * SLOT : 3 * SLOT, :] = picked[rows, :narrow]
         send[dest, 3 * SLOT :, :] = picked[rows, narrow:]
-    for load in loads:
-        load.wait()
+    load.wait()
 
 
 def weigh(ids, gates, select, weight):
@@ -157,7 +159,8 @@
     return [pl.ds(pl.multiple_of(at * half, half), half) for at in (group, 1 - group)]
 
 
-def teacher_in(own, other, gate, up, keep, send, rows, pre):
+def teacher_in(gate, up, own, other, keep, send, rows, pre, near, arrived):
+    loads = loads_of(arrived, (gate.at[0], near.at[0]), (up.at[0], near.at[1]))
     owners, _, narrow = own.shape
     replica = lax.axis_index("replica")
     for part, at in ((own, replica), (other, 1 - replica)):
@@ -166,8 +169,9 @@
             block = part[:, (2 + piece) * SLOT : (3 + piece) * SLOT, :]
             rows[:, pl.ds(start, narrow)] = block.reshape(owners * SLOT, narrow)
     mine, theirs = half_slices(pre.shape[0])
-    for index, matrix in enumerate((gate, up)):
-        pre[...] = contract(rows[...], matrix[0], (1, 1))
+    for index, load in enumerate(loads):
+        load.wait()
+        pre[...] = contract(rows[...], near[index], (1, 1))
         keep[index] = pre[mine, :]
         send[index] = pre[theirs, :].astype(BF16)
 
@@ -252,24 +256,41 @@
     out[0] = contract(hidden[...], rows[...], (0, 0)).astype(BF16)
 
 
-def slopes(own, diagonal, group, expert, out):
-    pieces = quad_slices(out.shape[1])
-    for piece, part in zip(pieces, (own, diagonal, group, expert)):
-        gate, up = part[0].astype(F32), part[1].astype(F32)
-        sig = jax.nn.sigmoid(gate)
-        out[0, piece, :] = up * sig * (1.0 + gate * (1.0 - sig))
-        out[1, piece, :] = gate * sig
-
-
-def grads(slope, a_own, a_got, b_own, b_got, rows, gate_out, up_out, left):
+def stack(own, got, both):
+    quarter = own.shape[1]
+    both[:, :quarter, :] = own[...]
+    both[:, quarter:, :] = got[...]
+
+
+def slopes(both, got, out):
+    quarter = both.shape[1] // 2
+    mine, diagonal, group, expert = quad_slices(out.shape[1])
+    for part, first, second in ((both, mine, expert), (got, group, diagonal)):
+        for at, piece in enumerate((first, second)):
+            rows = slice(at * quarter, (at + 1) * quarter)
+            gate, up = part[0, rows, :].astype(F32), part[1, rows, :].astype(F32)
+            sig = jax.nn.sigmoid(gate)
+            out[0, piece, :] = up * sig * (1.0 + gate * (1.0 - sig))
+            out[1, piece, :] = gate * sig
+
+
+def grads(slope, a_own, a_got, b_own, b_got, rows, gate_out, up_out, left, done, leaving):
     half = a_own.shape[0]
     for at, (own, got) in enumerate(((a_own, a_got), (b_own, b_got))):
         back = own[...].astype(F32) + got[...].astype(F32)
         block = slice(at * half, (at + 1) * half)
         for index in range(2):
             left[index, block, :] = (back * slope[index, block, :]).astype(BF16)
-    gate_out[0] = contract(left[0], rows[...], (0, 0)).astype(BF16)
-    up_out[0] = contract(left[1], rows[...], (0, 0)).astype(BF16)
+    copies = []
+    for index, out in enumerate((gate_out, up_out)):
+        for start in range(0, left.shape[2], TILE):
+            tile = slice(start, start + TILE)
+            done[index, tile, :] = contract(left[index, :, tile], rows[...], (0, 0)).astype(BF16)
+            semaphore = leaving.at[len(copies)]
+            copies.append(pltpu.make_async_copy(done.at[index, tile], out.at[0, tile], semaphore))
+            copies[-1].start()
+    for copy in copies:
+        copy.wait()
 
 
 def sum_bf16(own, got):
@@ -284,18 +305,17 @@
     narrow = width // 2
     slots = owners * SLOT
     full = 2 * slots
-    send, select, gate_near, up_near = call(
+    send, select, up_near = call(
         route,
         [
             struct(BF16, owners, 4 * SLOT, narrow),
             struct(BF16, slots, count),
             struct(BF16, 1, units, width),
-            struct(BF16, 1, units, width),
         ],
-        [member_order, stud_gate, stud_up, expert_ids.T, tokens],
-        [pltpu.VMEM((slots, block), BF16), pltpu.SemaphoreType.DMA((2,))],
+        [member_order, stud_up, expert_ids.T, tokens],
+        [pltpu.VMEM((slots, block), BF16), pltpu.SemaphoreType.DMA],
         smem=1,
-        far=2,
+        far=1,
         flops=2 * slots * count * block,
         space=pltpu.HBM,
     )
@@ -307,7 +327,7 @@
     keep, *parts, stud_rows = call(
         student_in,
         [struct(F32, 2, quarter, units), *pieces, struct(BF16, full, width)],
-        [own, other, gate_near, up_near],
+        [own, other, stud_gate, up_near],
         [pltpu.VMEM((full, units), F32)],
         flops=4 * full * width * units,
     )
@@ -316,8 +336,14 @@
     teach_keep, teach_send = call(
         teacher_in,
         [struct(F32, 2, half, units), struct(BF16, 2, half, units)],
-        [own, other, teach_gate, teach_up],
-        [pltpu.VMEM((slots, half_width), BF16), pltpu.VMEM((slots, units), F32)],
+        [teach_gate, teach_up, own, other],
+        [
+            pltpu.VMEM((slots, half_width), BF16),
+            pltpu.VMEM((slots, units), F32),
+            pltpu.VMEM((2, units, half_width), BF16),
+            pltpu.SemaphoreType.DMA((2,)),
+        ],
+        far=2,
         flops=4 * slots * half_width * units,
     )
     teach_got = swap(teach_send, "group")
@@ -329,7 +355,8 @@
         [keep, *parts],
     )
     hidden_parts = (hidden_piece, *quad(*[hidden_piece] * 3))
-    pre_parts = (pre, *quad(*[pre] * 3))
+    (pre_both,) = call(stack, [struct(BF16, 2, 2 * quarter, units)], [pre, swap(pre, "expert")])
+    pre_got = swap(pre_both, "group")
     teach_keep, teach_send = call(
         teacher_out,
         [struct(F32, slots, block), struct(BF16, slots, block)],
@@ -379,12 +406,17 @@
     back_second = sum_bf16(back_second, back_second_one)
     back_first_two = swap(back_first, "expert")
     back_second_two = swap(back_second, "group")
-    (slope,) = call(slopes, [struct(F32, 2, full, units)], [*pre_parts])
+    (slope,) = call(slopes, [struct(F32, 2, full, units)], [pre_both, pre_got])
     grad_gate, grad_up = call(
         grads,
         [result(BF16, 1, units, width), result(BF16, 1, units, width)],
         [slope, back_first, back_first_two, back_second, back_second_two, stud_rows],
-        [pltpu.VMEM((2, full, units), BF16)],
+        [
+            pltpu.VMEM((2, full, units), BF16),
+            pltpu.VMEM((2, units, width), BF16),
+            pltpu.SemaphoreType.DMA((2 * -(-units // TILE),)),
+        ],
+        far_outs=2,
         flops=4 * full * width * units,
     )
     return (residual, grad_gate, grad_up, grad_down)

time: 119 us -> 117 us (0.983)
  starting transfers between devices: 22.8 us -> 20.7 us
  local copies, waits for them, and re-layouts: 2.79 us -> 0.9 us
  Pallas kernels: 15.4 us -> 17 us
    unnamed x13 -> x11, local copies, waits for them, and re-layouts: 2.79 us -> 0.9 us
    pallas_call x14 -> x15, Pallas kernels: 15.4 us -> 17 us  [call(): pl.pallas_call(body, out_shape=outs, in_specs=specs, out_specs=[pl.BlockS...]
    ppermute x16, starting transfers between devices: 16.7 us -> 15.2 us  [swap(): lax.ppermute(block, axis, [(place, place ^ 1) for place in range(count)])]
    ppermute x3 -> x2, starting transfers between devices: 2.6 us -> 2.03 us  [quad(): diagonal = lax.ppermute(diagonal, ('expert', 'group'), crossing)]
    ppermute x3 -> x2, waiting for transfers between devices: 5.88 us -> 5.87 us  [quad(): diagonal = lax.ppermute(diagonal, ('expert', 'group'), crossing)]
  transfers between devices with their start and end apart: 20 -> 19, of which waited for: 13 -> 13; matrix products, arithmetic and copies ran while one was open for 1% -> 1% of each run, Pallas kernels for 4% -> 5%
where the time goes in v1:
time: 117 us; the launch traced here: 116 us
  waiting for transfers between devices  42.7 us (36%)
  blocking collectives  34.2 us (29%)
  starting transfers between devices  20.7 us (18%)
  Pallas kernels  17 us (15%)
    all_to_all x2, blocking collectives, exchange(): lax.all_to_all(block, 'expert', split_axis=0, concat_axis=0, tiled=True)  34.2 us
    ppermute x16, waiting for transfers between devices, swap(): lax.ppermute(block, axis, [(place, place ^ 1) for place in range(count)])  22 us
    pallas_call x15, Pallas kernels, call(): pl.pallas_call(body, out_shape=outs, in_specs=specs, out_specs=[pl.BlockS...  17 us
    ppermute x16, starting transfers between devices, swap(): lax.ppermute(block, axis, [(place, place ^ 1) for place in range(count)])  15.2 us
    all_to_all x1, waiting for transfers between devices, exchange(): lax.all_to_all(block, 'expert', split_axis=0, concat_axis=0, tiled=True)  14.8 us
    ppermute x2, waiting for transfers between devices, quad(): diagonal = lax.ppermute(diagonal, ('expert', 'group'), crossing)  5.87 us
    all_to_all x1, starting transfers between devices, exchange(): lax.all_to_all(block, 'expert', split_axis=0, concat_axis=0, tiled=True)  3.49 us
  transfers between devices with their start and end apart: 19, of which 13 were waited for; matrix products, arithmetic and copies ran while one was open for 1% of the time, Pallas kernels for 5%

profile of v1, /device:TPU:0, one launch (start us, length us, event | category | flops | bytes accessed | tf_op | source)
XLA Modules:
  0.0 116.4 jit_solution(7547262675045776487)
XLA Ops:
  0.6 2.6 %shard_map.129 = (bf16[8,64,512]{2,1,0:T(8,128)(2,1)S(1)}, bf16[128,192]{1,0:T(8,128)(2,1)S(1)}, bf16[1,768,1024]{2,1,0:T(8,128)(2,1)S(1)}) custom-call(s32[8]{0:T(128)} %order.3, bf16[1,768,1024]{2,1,0:T(8,128)(2,1)} %up_hbm.1, s32[8,192]{1,0:T(8,128)} %bitcast.2, bf16[192,2048]{1,0:T(8,128)(2,1)} %tokens.1), custom_call_target="tpu_custom_call" | custom-call | flops 50331648 | bytes 2365472 | tf_op jit(solution)/shard_map/pallas_call | solution.py:44
  3.2 21.6 %all_to_all.15.own = bf16[8,64,512]{2,1,0:T(8,128)(2,1)S(1)} all-to-all(bf16[8,64,512]{2,1,0:T(8,128)(2,1)S(1)} %get-tuple-element.28), channel_id=1, replica_groups=mesh['expert'=8,'replica'=2,'group'=2] {'expert'}, dimensions={0} | all-to-all | bytes 1048576 | tf_op jit(solution)/shard_map/all_to_all | solution.py:30
  24.9 0.0 copy-start.2
  24.9 0.0 collective-permute-start
  24.9 1.9 %collective-permute-done.other = bf16[8,64,512]{2,1,0:T(8,128)(2,1)S(1)} collective-permute-done((bf16[8,64,512]{2,1,0:T(8,128)(2,1)S(1)}, bf16[8,64,512]{2,1,0:T(8,128)(2,1)S(1)}, u32[]{:S(2)}, u32[]{:S(2)}) %collective-permute-start) | collective-permute-done | bytes 524320 | tf_op jit(solution)/shard_map/ppermute | solution.py:19
  26.8 4.7 %shard_map.133 = (f32[2,64,768]{2,1,0:T(8,128)S(1)}, bf16[2,64,768]{2,1,0:T(8,128)(2,1)S(1)}) custom-call(bf16[1,768,2048]{2,1,0:T(8,128)(2,1)} %gate.3, bf16[1,768,2048]{2,1,0:T(8,128)(2,1)} %up.1, bf16[8,64,512]{2,1,0:T(8,128)(2,1)S(1)} %all_to_all.15.own, bf16[8,64,512]{2,1,0:T(8,128)(2,1)S(1)} %collective-permute-done.other), custom_call_target="tpu_custom_call" | custom-call | flops 805306368 | bytes 7340032 | tf_op jit(solution)/shard_map/pallas_call | solution.py:44
  31.5 1.6 %collective-permute-start.8 = (bf16[2,64,768]{2,1,0:T(8,128)(2,1)S(1)}, bf16[2,64,768]{2,1,0:T(8,128)(2,1)S(1)}, u32[]{:S(2)}, u32[]{:S(2)}) collective-permute-start(bf16[2,64,768]{2,1,0:T(8,128)(2,1)S(1)} %get-tuple-element.38), channel_id=1, source_target_pairs={{0,1},{1,0},{2,3},{3,2},{4,5},{5,4},{6,7},{7,6},{8,9},{9,8},{10,11... | collective-permute-start | bytes 589832 | tf_op jit(solution)/shard_map/ppermute | solution.py:19
  33.1 0.0 copy-done.2
  33.1 0.0 copy-start.1
  33.1 1.1 shard_map.130
  34.2 1.5 %collective-permute-start.1 = (bf16[2,64,768]{2,1,0:T(8,128)(2,1)S(1)}, bf16[2,64,768]{2,1,0:T(8,128)(2,1)S(1)}, u32[]{:S(2)}, u32[]{:S(2)}) collective-permute-start(bf16[2,64,768]{2,1,0:T(8,128)(2,1)S(1)} %get-tuple-element.31), channel_id=1, source_target_pairs={{0,5},{1,4},{4,1},{5,0},{8,13},{9,12},{12,9},{13,8},{16,21},{17,20... | collective-permute-start | bytes 589832 | tf_op jit(solution)/shard_map/ppermute | solution.py:25
  35.6 1.5 %collective-permute-start.2 = (bf16[2,64,768]{2,1,0:T(8,128)(2,1)S(1)}, bf16[2,64,768]{2,1,0:T(8,128)(2,1)S(1)}, u32[]{:S(2)}, u32[]{:S(2)}) collective-permute-start(bf16[2,64,768]{2,1,0:T(8,128)(2,1)S(1)} %get-tuple-element.32), channel_id=1, source_target_pairs={{0,1},{1,0},{2,3},{3,2},{4,5},{5,4},{6,7},{7,6},{8,9},{9,8},{10,11... | collective-permute-start | bytes 589832 | tf_op jit(solution)/shard_map/ppermute | solution.py:19
  37.1 0.6 collective-permute-start.3
  37.7 1.6 %collective-permute-done.8.got = bf16[2,64,768]{2,1,0:T(8,128)(2,1)S(1)} collective-permute-done((bf16[2,64,768]{2,1,0:T(8,128)(2,1)S(1)}, bf16[2,64,768]{2,1,0:T(8,128)(2,1)S(1)}, u32[]{:S(2)}, u32[]{:S(2)}) %collective-permute-start.8) | collective-permute-done | bytes 196640 | tf_op jit(solution)/shard_map/ppermute | solution.py:19
  39.4 0.1 shard_map.134.own
  39.4 1.6 %collective-permute-start.9 = (bf16[64,768]{1,0:T(8,128)(2,1)S(1)}, bf16[64,768]{1,0:T(8,128)(2,1)S(1)}, u32[]{:S(2)}, u32[]{:S(2)}) collective-permute-start(bf16[64,768]{1,0:T(8,128)(2,1)S(1)} %shard_map.134.own), channel_id=1, source_target_pairs={{0,1},{1,0},{2,3},{3,2},{4,5},{5,4},{6,7},{7,6},{8,9},{9,8},{10,11... | collective-permute-start | bytes 294920 | tf_op jit(solution)/shard_map/ppermute | solution.py:19
  41.0 3.5 %collective-permute-done.1.diagonal = bf16[2,64,768]{2,1,0:T(8,128)(2,1)S(1)} collective-permute-done((bf16[2,64,768]{2,1,0:T(8,128)(2,1)S(1)}, bf16[2,64,768]{2,1,0:T(8,128)(2,1)S(1)}, u32[]{:S(2)}, u32[]{:S(2)}) %collective-permute-start.1) | collective-permute-done | bytes 196640 | tf_op jit(solution)/shard_map/ppermute | solution.py:25
  44.5 3.4 %collective-permute-done.2.group = bf16[2,64,768]{2,1,0:T(8,128)(2,1)S(1)} collective-permute-done((bf16[2,64,768]{2,1,0:T(8,128)(2,1)S(1)}, bf16[2,64,768]{2,1,0:T(8,128)(2,1)S(1)}, u32[]{:S(2)}, u32[]{:S(2)}) %collective-permute-start.2) | collective-permute-done | bytes 196640 | tf_op jit(solution)/shard_map/ppermute | solution.py:19
  47.8 0.0 collective-permute-done.3.expert
  47.8 0.1 shard_map.131
  48.0 0.0 copy-start
  48.0 1.5 %collective-permute-start.6 = (bf16[64,768]{1,0:T(8,128)(2,1)S(1)}, bf16[64,768]{1,0:T(8,128)(2,1)S(1)}, u32[]{:S(2)}, u32[]{:S(2)}) collective-permute-start(bf16[64,768]{1,0:T(8,128)(2,1)S(1)} %get-tuple-element.34.own), channel_id=1, source_target_pairs={{0,4},{4,0},{8,12},{12,8},{16,20},{20,16},{24,28},{28,24},{1,5},{5... | collective-permute-start | bytes 294920 | tf_op jit(solution)/shard_map/ppermute | solution.py:19
  49.5 1.5 %collective-permute-start.5 = (bf16[64,768]{1,0:T(8,128)(2,1)S(1)}, bf16[64,768]{1,0:T(8,128)(2,1)S(1)}, u32[]{:S(2)}, u32[]{:S(2)}) collective-permute-start(bf16[64,768]{1,0:T(8,128)(2,1)S(1)} %get-tuple-element.34.own), channel_id=1, source_target_pairs={{0,1},{1,0},{2,3},{3,2},{4,5},{5,4},{6,7},{7,6},{8,9},{9,8},{10,11... | collective-permute-start | bytes 294920 | tf_op jit(solution)/shard_map/ppermute | solution.py:19
  50.9 0.6 collective-permute-start.4
  51.5 0.0 collective-permute-done.9.got
  51.5 0.0 copy-done.1
  51.5 0.6 shard_map.135
  52.1 0.1 collective-permute-start.10
  52.2 1.4 %collective-permute-done.6.expert = bf16[64,768]{1,0:T(8,128)(2,1)S(1)} collective-permute-done((bf16[64,768]{1,0:T(8,128)(2,1)S(1)}, bf16[64,768]{1,0:T(8,128)(2,1)S(1)}, u32[]{:S(2)}, u32[]{:S(2)}) %collective-permute-start.6) | collective-permute-done | bytes 98336 | tf_op jit(solution)/shard_map/ppermute | solution.py:19
  53.6 0.4 collective-permute-done.5.group
  54.1 2.4 %collective-permute-done.4.diagonal = bf16[64,768]{1,0:T(8,128)(2,1)S(1)} collective-permute-done((bf16[64,768]{1,0:T(8,128)(2,1)S(1)}, bf16[64,768]{1,0:T(8,128)(2,1)S(1)}, u32[]{:S(2)}, u32[]{:S(2)}) %collective-permute-start.4) | collective-permute-done | bytes 98336 | tf_op jit(solution)/shard_map/ppermute | solution.py:25
  56.5 0.0 copy-done
  56.5 0.6 shard_map.132
  57.1 0.1 collective-permute-start.7
  57.1 0.0 collective-permute-done.10.teach_got
  57.2 1.5 %collective-permute-done.7.stud_got = bf16[256,512]{1,0:T(8,128)(2,1)S(1)} collective-permute-done((bf16[256,512]{1,0:T(8,128)(2,1)S(1)}, bf16[256,512]{1,0:T(8,128)(2,1)S(1)}, u32[]{:S(2)}, u32[]{:S(2)}) %collective-permute-start.7) | collective-permute-done | bytes 262176 | tf_op jit(solution)/shard_map/ppermute | solution.py:19
  58.7 0.0 copy-start.3
  58.7 0.9 shard_map.136
  59.6 3.5 %all-to-all-start.1 = ((bf16[8,64,512]{2,1,0:T(8,128)(2,1)}), bf16[8,64,512]{2,1,0:T(8,128)(2,1)S(1)}, u32[]{:S(2)}, u32[]{:S(2)}) async-start(bf16[8,64,512]{2,1,0:T(8,128)(2,1)} %shard_map.136), calls=%async_computation.1 | async-start | bytes 1048576 | tf_op jit(solution)/shard_map/all_to_all | solution.py:30
  63.1 0.0 copy-done.3
  63.1 0.0 copy-done.4
  63.1 0.2 shard_map.137.weight
  63.2 14.8 %all-to-all-done.1.back = bf16[8,64,512]{2,1,0:T(8,128)(2,1)S(1)} async-done(((bf16[8,64,512]{2,1,0:T(8,128)(2,1)}), bf16[8,64,512]{2,1,0:T(8,128)(2,1)S(1)}, u32[]{:S(2)}, u32[]{:S(2)}) %all-to-all-start.1) | async-done | bytes 524320 | tf_op jit(solution)/shard_map/all_to_all | solution.py:30
  78.0 1.4 %shard_map.138 = (f32[192,1024]{1,0:T(8,128)S(1)}, bf16[8,32,512]{2,1,0:T(8,128)(2,1)S(1)}) custom-call(s32[8]{0:T(128)} %order.3, bf16[8,64,512]{2,1,0:T(8,128)(2,1)S(1)} %all-to-all-done.1.back, bf16[128,192]{1,0:T(8,128)(2,1)S(1)} %get-tuple-element.41.select, f32[128,1]{1,0:T(8,128)S(1)} %shard_map.137.weight), custom_call_target="tpu_custom_call" | custom-call | flops 201326592 | bytes 573984 | tf_op jit(solution)/shard_map/pallas_call | solution.py:44
  79.4 12.5 %all_to_all.16.own = bf16[8,32,512]{2,1,0:T(8,128)(2,1)S(1)} all-to-all(bf16[8,32,512]{2,1,0:T(8,128)(2,1)S(1)} %get-tuple-element.44), channel_id=1, replica_groups=mesh['expert'=8,'replica'=2,'group'=2] {'expert'}, dimensions={0} | all-to-all | bytes 524288 | tf_op jit(solution)/shard_map/all_to_all | solution.py:30
  92.0 0.0 collective-permute-start.13
  92.0 1.4 %collective-permute-start.11 = (bf16[2,64,768]{2,1,0:T(8,128)(2,1)S(1)}, bf16[2,64,768]{2,1,0:T(8,128)(2,1)S(1)}, u32[]{:S(2)}, u32[]{:S(2)}) collective-permute-start(bf16[2,64,768]{2,1,0:T(8,128)(2,1)S(1)} %get-tuple-element.43.own), channel_id=1, source_target_pairs={{0,4},{4,0},{8,12},{12,8},{16,20},{20,16},{24,28},{28,24},{1,5},{5... | collective-permute-start | bytes 589832 | tf_op jit(solution)/shard_map/ppermute | solution.py:19
  93.4 0.1 collective-permute-done.13.other
  93.5 0.6 shard_map.141
  94.1 0.6 collective-permute-start.14
  94.7 4.6 %collective-permute-done.11.got = bf16[2,64,768]{2,1,0:T(8,128)(2,1)S(1)} collective-permute-done((bf16[2,64,768]{2,1,0:T(8,128)(2,1)S(1)}, bf16[2,64,768]{2,1,0:T(8,128)(2,1)S(1)}, u32[]{:S(2)}, u32[]{:S(2)}) %collective-permute-start.11) | collective-permute-done | bytes 196640 | tf_op jit(solution)/shard_map/ppermute | solution.py:19
  99.3 0.6 collective-permute-start.12
  99.9 1.4 %collective-permute-start.16 = (bf16[128,768]{1,0:T(8,128)(2,1)S(1)}, bf16[128,768]{1,0:T(8,128)(2,1)S(1)}, u32[]{:S(2)}, u32[]{:S(2)}) collective-permute-start(bf16[128,768]{1,0:T(8,128)(2,1)S(1)} %get-tuple-element.46), channel_id=1, source_target_pairs={{0,4},{4,0},{8,12},{12,8},{16,20},{20,16},{24,28},{28,24},{1,5},{5... | collective-permute-start | bytes 589832 | tf_op jit(solution)/shard_map/ppermute | solution.py:19
  101.3 0.0 collective-permute-done.14
  101.4 1.3 %collective-permute-start.15 = (bf16[128,768]{1,0:T(8,128)(2,1)S(1)}, bf16[128,768]{1,0:T(8,128)(2,1)S(1)}, u32[]{:S(2)}, u32[]{:S(2)}) collective-permute-start(bf16[128,768]{1,0:T(8,128)(2,1)S(1)} %add_convert_fusion.1.a_own), channel_id=1, source_target_pairs={{0,4},{4,0},{8,12},{12,8},{16,20},{20,16},{24,28},{28,24},{1,5},{5... | collective-permute-start | bytes 589832 | tf_op jit(solution)/shard_map/ppermute | solution.py:19
  102.7 5.0 %collective-permute-done.16 = bf16[128,768]{1,0:T(8,128)(2,1)S(1)} collective-permute-done((bf16[128,768]{1,0:T(8,128)(2,1)S(1)}, bf16[128,768]{1,0:T(8,128)(2,1)S(1)}, u32[]{:S(2)}, u32[]{:S(2)}) %collective-permute-start.16) | collective-permute-done | bytes 196640 | tf_op jit(solution)/shard_map/ppermute | solution.py:19
  107.7 1.6 %collective-permute-start.17 = (bf16[128,768]{1,0:T(8,128)(2,1)S(1)}, bf16[128,768]{1,0:T(8,128)(2,1)S(1)}, u32[]{:S(2)}, u32[]{:S(2)}) collective-permute-start(bf16[128,768]{1,0:T(8,128)(2,1)S(1)} %add_convert_fusion.b_own), channel_id=1, source_target_pairs={{0,1},{1,0},{2,3},{3,2},{4,5},{5,4},{6,7},{7,6},{8,9},{9,8},{10,11... | collective-permute-start | bytes 589832 | tf_op jit(solution)/shard_map/ppermute | solution.py:19
  109.3 2.1 %collective-permute-done.12.got = bf16[2,128,768]{2,1,0:T(8,128)(2,1)S(1)} collective-permute-done((bf16[2,128,768]{2,1,0:T(8,128)(2,1)S(1)}, bf16[2,128,768]{2,1,0:T(8,128)(2,1)S(1)}, u32[]{:S(2)}, u32[]{:S(2)}) %collective-permute-start.12) | collective-permute-done | bytes 393248 | tf_op jit(solution)/shard_map/ppermute | solution.py:19
  111.4 0.3 shard_map.140.slope
  111.7 0.9 copy.14
  112.6 1.7 %shard_map.143 = bf16[1,768,1024]{2,1,0:T(8,128)(2,1)} custom-call(bf16[256,768]{1,0:T(8,128)(2,1)S(1)} %get-tuple-element.50.hidden, bf16[256,1024]{1,0:T(8,128)(2,1)S(1)} %get-tuple-element.51.rows), custom_call_target="tpu_custom_call" | custom-call | flops 402653184 | bytes 917504 | tf_op jit(solution)/shard_map/pallas_call | solution.py:44
  114.3 0.0 collective-permute-done.15.a_got
  114.3 0.0 collective-permute-done.17.b_got
  114.3 2.1 %shard_map.142 = (bf16[1,768,1024]{2,1,0:T(8,128)(2,1)}, bf16[1,768,1024]{2,1,0:T(8,128)(2,1)}) custom-call(f32[2,256,768]{2,1,0:T(8,128)S(1)} %shard_map.140.slope, bf16[128,768]{1,0:T(8,128)(2,1)S(1)} %add_convert_fusion.1.a_own, bf16[128,768]{1,0:T(8,128)(2,1)S(1)} %collective-permute-done.15.a_got, bf16[128,768]{1,0:T(8,128)(2,1)S(1)} %add_convert_fusion.b_own, ...), custom_call_target="tpu_custom_call" | custom-call | flops 805306368 | bytes 2883584 | tf_op jit(solution)/shard_map/pallas_call | solution.py:44
  (4 shorter events, 0.1 us)
Async XLA Ops:
  24.9 8.2 %copy-start.2 = (bf16[1,768,1024]{2,1,0:T(8,128)(2,1)S(1)}, bf16[1,768,1024]{2,1,0:T(8,128)(2,1)}, u32[]{:S(2)}) copy-start(bf16[1,768,1024]{2,1,0:T(8,128)(2,1)} %gate.2) | copy-start | bytes 4718596
  24.9 1.9 %collective-permute-start = (bf16[8,64,512]{2,1,0:T(8,128)(2,1)S(1)}, bf16[8,64,512]{2,1,0:T(8,128)(2,1)S(1)}, u32[]{:S(2)}, u32[]{:S(2)}) collective-permute-start(bf16[8,64,512]{2,1,0:T(8,128)(2,1)S(1)} %all_to_all.15.own), channel_id=1, source_target_pairs={{0,2},{2,0},{1,3},{3,1},{4,6},{6,4},{5,7},{7,5},{8,10},{10,8},{9,1... | collective-permute-start | bytes 1572872 | tf_op jit(solution)/shard_map/ppermute | solution.py:19
  31.5 7.8 %collective-permute-start.8 = (bf16[2,64,768]{2,1,0:T(8,128)(2,1)S(1)}, bf16[2,64,768]{2,1,0:T(8,128)(2,1)S(1)}, u32[]{:S(2)}, u32[]{:S(2)}) collective-permute-start(bf16[2,64,768]{2,1,0:T(8,128)(2,1)S(1)} %get-tuple-element.38), channel_id=1, source_target_pairs={{0,1},{1,0},{2,3},{3,2},{4,5},{5,4},{6,7},{7,6},{8,9},{9,8},{10,11... | collective-permute-start | bytes 589832 | tf_op jit(solution)/shard_map/ppermute | solution.py:19
  33.1 18.4 %copy-start.1 = (bf16[1,768,2048]{2,1,0:T(8,128)(2,1)S(1)}, bf16[1,768,2048]{2,1,0:T(8,128)(2,1)}, u32[]{:S(2)}) copy-start(bf16[1,768,2048]{2,1,0:T(8,128)(2,1)} %down.4) | copy-start | bytes 9437188
  34.2 10.3 %collective-permute-start.1 = (bf16[2,64,768]{2,1,0:T(8,128)(2,1)S(1)}, bf16[2,64,768]{2,1,0:T(8,128)(2,1)S(1)}, u32[]{:S(2)}, u32[]{:S(2)}) collective-permute-start(bf16[2,64,768]{2,1,0:T(8,128)(2,1)S(1)} %get-tuple-element.31), channel_id=1, source_target_pairs={{0,5},{1,4},{4,1},{5,0},{8,13},{9,12},{12,9},{13,8},{16,21},{17,20... | collective-permute-start | bytes 589832 | tf_op jit(solution)/shard_map/ppermute | solution.py:25
  35.6 12.2 %collective-permute-start.2 = (bf16[2,64,768]{2,1,0:T(8,128)(2,1)S(1)}, bf16[2,64,768]{2,1,0:T(8,128)(2,1)S(1)}, u32[]{:S(2)}, u32[]{:S(2)}) collective-permute-start(bf16[2,64,768]{2,1,0:T(8,128)(2,1)S(1)} %get-tuple-element.32), channel_id=1, source_target_pairs={{0,1},{1,0},{2,3},{3,2},{4,5},{5,4},{6,7},{7,6},{8,9},{9,8},{10,11... | collective-permute-start | bytes 589832 | tf_op jit(solution)/shard_map/ppermute | solution.py:19
  37.1 10.7 %collective-permute-start.3 = (bf16[2,64,768]{2,1,0:T(8,128)(2,1)S(1)}, bf16[2,64,768]{2,1,0:T(8,128)(2,1)S(1)}, u32[]{:S(2)}, u32[]{:S(2)}) collective-permute-start(bf16[2,64,768]{2,1,0:T(8,128)(2,1)S(1)} %get-tuple-element.33), channel_id=1, source_target_pairs={{0,4},{4,0},{8,12},{12,8},{16,20},{20,16},{24,28},{28,24},{1,5},{5... | collective-permute-start | bytes 589832 | tf_op jit(solution)/shard_map/ppermute | solution.py:19
  39.4 12.1 %collective-permute-start.9 = (bf16[64,768]{1,0:T(8,128)(2,1)S(1)}, bf16[64,768]{1,0:T(8,128)(2,1)S(1)}, u32[]{:S(2)}, u32[]{:S(2)}) collective-permute-start(bf16[64,768]{1,0:T(8,128)(2,1)S(1)} %shard_map.134.own), channel_id=1, source_target_pairs={{0,1},{1,0},{2,3},{3,2},{4,5},{5,4},{6,7},{7,6},{8,9},{9,8},{10,11... | collective-permute-start | bytes 294920 | tf_op jit(solution)/shard_map/ppermute | solution.py:19
  48.0 8.5 %copy-start = (bf16[1,768,1024]{2,1,0:T(8,128)(2,1)S(1)}, bf16[1,768,1024]{2,1,0:T(8,128)(2,1)}, u32[]{:S(2)}) copy-start(bf16[1,768,1024]{2,1,0:T(8,128)(2,1)} %down.5) | copy-start | bytes 4718596
  48.0 5.7 %collective-permute-start.6 = (bf16[64,768]{1,0:T(8,128)(2,1)S(1)}, bf16[64,768]{1,0:T(8,128)(2,1)S(1)}, u32[]{:S(2)}, u32[]{:S(2)}) collective-permute-start(bf16[64,768]{1,0:T(8,128)(2,1)S(1)} %get-tuple-element.34.own), channel_id=1, source_target_pairs={{0,4},{4,0},{8,12},{12,8},{16,20},{20,16},{24,28},{28,24},{1,5},{5... | collective-permute-start | bytes 294920 | tf_op jit(solution)/shard_map/ppermute | solution.py:19
  49.5 4.6 %collective-permute-start.5 = (bf16[64,768]{1,0:T(8,128)(2,1)S(1)}, bf16[64,768]{1,0:T(8,128)(2,1)S(1)}, u32[]{:S(2)}, u32[]{:S(2)}) collective-permute-start(bf16[64,768]{1,0:T(8,128)(2,1)S(1)} %get-tuple-element.34.own), channel_id=1, source_target_pairs={{0,1},{1,0},{2,3},{3,2},{4,5},{5,4},{6,7},{7,6},{8,9},{9,8},{10,11... | collective-permute-start | bytes 294920 | tf_op jit(solution)/shard_map/ppermute | solution.py:19
  50.9 5.5 %collective-permute-start.4 = (bf16[64,768]{1,0:T(8,128)(2,1)S(1)}, bf16[64,768]{1,0:T(8,128)(2,1)S(1)}, u32[]{:S(2)}, u32[]{:S(2)}) collective-permute-start(bf16[64,768]{1,0:T(8,128)(2,1)S(1)} %get-tuple-element.34.own), channel_id=1, source_target_pairs={{0,5},{1,4},{4,1},{5,0},{8,13},{9,12},{12,9},{13,8},{16,21},{17,20... | collective-permute-start | bytes 294920 | tf_op jit(solution)/shard_map/ppermute | solution.py:25
  52.1 5.0 %collective-permute-start.10 = (bf16[128,1024]{1,0:T(8,128)(2,1)S(1)}, bf16[128,1024]{1,0:T(8,128)(2,1)S(1)}, u32[]{:S(2)}, u32[]{:S(2)}) collective-permute-start(bf16[128,1024]{1,0:T(8,128)(2,1)S(1)} %get-tuple-element.40), channel_id=1, source_target_pairs={{0,2},{2,0},{1,3},{3,1},{4,6},{6,4},{5,7},{7,5},{8,10},{10,8},{9,1... | collective-permute-start | bytes 786440 | tf_op jit(solution)/shard_map/ppermute | solution.py:19
  57.1 1.6 %collective-permute-start.7 = (bf16[256,512]{1,0:T(8,128)(2,1)S(1)}, bf16[256,512]{1,0:T(8,128)(2,1)S(1)}, u32[]{:S(2)}, u32[]{:S(2)}) collective-permute-start(bf16[256,512]{1,0:T(8,128)(2,1)S(1)} %get-tuple-element.36), channel_id=1, source_target_pairs={{0,2},{2,0},{1,3},{3,1},{4,6},{6,4},{5,7},{7,5},{8,10},{10,8},{9,1... | collective-permute-start | bytes 786440 | tf_op jit(solution)/shard_map/ppermute | solution.py:19
  58.7 4.4 %copy-start.3 = (s32[192,8]{0,1:T(8,128)S(1)}, s32[192,8]{0,1:T(8,128)}, u32[]{:S(2)}) copy-start(s32[192,8]{0,1:T(8,128)} %param.11) | copy-start | bytes 18436
  58.7 4.4 %copy-start.4 = (f32[192,8]{0,1:T(8,128)S(1)}, f32[192,8]{0,1:T(8,128)}, u32[]{:S(2)}) copy-start(f32[192,8]{0,1:T(8,128)} %param.12) | copy-start | bytes 18436
  59.6 18.5 %all-to-all-start.1 = ((bf16[8,64,512]{2,1,0:T(8,128)(2,1)}), bf16[8,64,512]{2,1,0:T(8,128)(2,1)S(1)}, u32[]{:S(2)}, u32[]{:S(2)}) async-start(bf16[8,64,512]{2,1,0:T(8,128)(2,1)} %shard_map.136), calls=%async_computation.1 | async-start | bytes 1048576 | tf_op jit(solution)/shard_map/all_to_all | solution.py:30
  92.0 1.5 %collective-permute-start.13 = (bf16[8,32,512]{2,1,0:T(8,128)(2,1)S(1)}, bf16[8,32,512]{2,1,0:T(8,128)(2,1)S(1)}, u32[]{:S(2)}, u32[]{:S(2)}) collective-permute-start(bf16[8,32,512]{2,1,0:T(8,128)(2,1)S(1)} %all_to_all.16.own), channel_id=1, source_target_pairs={{0,2},{2,0},{1,3},{3,1},{4,6},{6,4},{5,7},{7,5},{8,10},{10,8},{9,1... | collective-permute-start | bytes 786440 | tf_op jit(solution)/shard_map/ppermute | solution.py:19
  92.0 7.3 %collective-permute-start.11 = (bf16[2,64,768]{2,1,0:T(8,128)(2,1)S(1)}, bf16[2,64,768]{2,1,0:T(8,128)(2,1)S(1)}, u32[]{:S(2)}, u32[]{:S(2)}) collective-permute-start(bf16[2,64,768]{2,1,0:T(8,128)(2,1)S(1)} %get-tuple-element.43.own), channel_id=1, source_target_pairs={{0,4},{4,0},{8,12},{12,8},{16,20},{20,16},{24,28},{28,24},{1,5},{5... | collective-permute-start | bytes 589832 | tf_op jit(solution)/shard_map/ppermute | solution.py:19
  94.1 7.2 %collective-permute-start.14 = (bf16[128,768]{1,0:T(8,128)(2,1)S(1)}, bf16[128,768]{1,0:T(8,128)(2,1)S(1)}, u32[]{:S(2)}, u32[]{:S(2)}) collective-permute-start(bf16[128,768]{1,0:T(8,128)(2,1)S(1)} %get-tuple-element.45), channel_id=1, source_target_pairs={{0,1},{1,0},{2,3},{3,2},{4,5},{5,4},{6,7},{7,6},{8,9},{9,8},{10,11... | collective-permute-start | bytes 589832 | tf_op jit(solution)/shard_map/ppermute | solution.py:19
  99.3 12.1 %collective-permute-start.12 = (bf16[2,128,768]{2,1,0:T(8,128)(2,1)S(1)}, bf16[2,128,768]{2,1,0:T(8,128)(2,1)S(1)}, u32[]{:S(2)}, u32[]{:S(2)}) collective-permute-start(bf16[2,128,768]{2,1,0:T(8,128)(2,1)S(1)} %shard_map.139.both), channel_id=1, source_target_pairs={{0,1},{1,0},{2,3},{3,2},{4,5},{5,4},{6,7},{7,6},{8,9},{9,8},{10,11... | collective-permute-start | bytes 1179656 | tf_op jit(solution)/shard_map/ppermute | solution.py:19
  99.9 7.8 %collective-permute-start.16 = (bf16[128,768]{1,0:T(8,128)(2,1)S(1)}, bf16[128,768]{1,0:T(8,128)(2,1)S(1)}, u32[]{:S(2)}, u32[]{:S(2)}) collective-permute-start(bf16[128,768]{1,0:T(8,128)(2,1)S(1)} %get-tuple-element.46), channel_id=1, source_target_pairs={{0,4},{4,0},{8,12},{12,8},{16,20},{20,16},{24,28},{28,24},{1,5},{5... | collective-permute-start | bytes 589832 | tf_op jit(solution)/shard_map/ppermute | solution.py:19
  101.4 12.9 %collective-permute-start.15 = (bf16[128,768]{1,0:T(8,128)(2,1)S(1)}, bf16[128,768]{1,0:T(8,128)(2,1)S(1)}, u32[]{:S(2)}, u32[]{:S(2)}) collective-permute-start(bf16[128,768]{1,0:T(8,128)(2,1)S(1)} %add_convert_fusion.1.a_own), channel_id=1, source_target_pairs={{0,4},{4,0},{8,12},{12,8},{16,20},{20,16},{24,28},{28,24},{1,5},{5... | collective-permute-start | bytes 589832 | tf_op jit(solution)/shard_map/ppermute | solution.py:19
  107.7 6.6 %collective-permute-start.17 = (bf16[128,768]{1,0:T(8,128)(2,1)S(1)}, bf16[128,768]{1,0:T(8,128)(2,1)S(1)}, u32[]{:S(2)}, u32[]{:S(2)}) collective-permute-start(bf16[128,768]{1,0:T(8,128)(2,1)S(1)} %add_convert_fusion.b_own), channel_id=1, source_target_pairs={{0,1},{1,0},{2,3},{3,2},{4,5},{5,4},{6,7},{7,6},{8,9},{9,8},{10,11... | collective-permute-start | bytes 589832 | tf_op jit(solution)/shard_map/ppermute | solution.py:19

commit v2 on v1

--- a/solution.py
+++ b/solution.py
@@ -86,10 +86,11 @@
     return [ids[choice : choice + 1, :] == expert for choice in range(ids.shape[0])]
 
 
-def route(order, up_hbm, ids, tokens, send, select, up_near, picked, arrived):
-    load = pltpu.make_async_copy(up_hbm, up_near, arrived)
-    load.start()
+def route(order, up_hbm, tokens_hbm, ids, send, select, up_near, picked, tokens, arrived):
     owners, _, narrow = send.shape
+    start = pl.multiple_of(lax.axis_index("replica") * 2 * narrow, 2 * narrow)
+    columns = tokens_hbm.at[:, pl.ds(start, 2 * narrow)]
+    loads = loads_of(arrived, (columns, tokens), (up_hbm, up_near))
     slots, count = select.shape
     slot = (lax.broadcasted_iota(jnp.int32, (slots, count), 0) % SLOT).astype(F32)
     member = jnp.zeros((slots, count), F32)
@@ -102,14 +103,14 @@
     chosen = (member > 0.0) & (rank == slot)
     onehot = jnp.where(chosen, 1.0, 0.0).astype(BF16)
     select[...] = onehot
-    start = pl.multiple_of(lax.axis_index("replica") * 2 * narrow, 2 * narrow)
-    picked[...] = contract(onehot, tokens[:, pl.ds(start, 2 * narrow)], (1, 0)).astype(BF16)
+    loads[0].wait()
+    picked[...] = contract(onehot, tokens[...], (1, 0)).astype(BF16)
     spread_members(order, picked, send, False)
     for dest in range(owners):
         rows = slice(dest * SLOT, (dest + 1) * SLOT)
         send[dest, 2 * SLOT : 3 * SLOT, :] = picked[rows, :narrow]
         send[dest, 3 * SLOT :, :] = picked[rows, narrow:]
-    load.wait()
+    loads[1].wait()
 
 
 def weigh(ids, gates, select, weight):
@@ -312,10 +313,10 @@
             struct(BF16, slots, count),
             struct(BF16, 1, units, width),
         ],
-        [member_order, stud_up, expert_ids.T, tokens],
-        [pltpu.VMEM((slots, block), BF16), pltpu.SemaphoreType.DMA],
+        [member_order, stud_up, tokens, expert_ids.T],
+        [pltpu.VMEM((slots, block), BF16), pltpu.VMEM((count, block), BF16), pltpu.SemaphoreType.DMA((2,))],
         smem=1,
-        far=1,
+        far=2,
         flops=2 * slots * count * block,
         space=pltpu.HBM,
     )

time: 117 us -> 116 us (level)
  no operation moved by 1% of the time
where the time goes in v2:
time: 116 us
  waiting for transfers between devices  42.7 us (37%)
  blocking collectives  34.2 us (29%)
  starting transfers between devices  20.7 us (18%)
  Pallas kernels  16.7 us (14%)
    all_to_all x2, blocking collectives, exchange(): lax.all_to_all(block, 'expert', split_axis=0, concat_axis=0, tiled=True)  34.2 us
    ppermute x16, waiting for transfers between devices, swap(): lax.ppermute(block, axis, [(place, place ^ 1) for place in range(count)])  22 us
    pallas_call x15, Pallas kernels, call(): pl.pallas_call(body, out_shape=outs, in_specs=specs, out_specs=[pl.BlockS...  16.7 us
    ppermute x16, starting transfers between devices, swap(): lax.ppermute(block, axis, [(place, place ^ 1) for place in range(count)])  15.2 us
    all_to_all x1, waiting for transfers between devices, exchange(): lax.all_to_all(block, 'expert', split_axis=0, concat_axis=0, tiled=True)  14.8 us
    ppermute x2, waiting for transfers between devices, quad(): diagonal = lax.ppermute(diagonal, ('expert', 'group'), crossing)  5.88 us
    all_to_all x1, starting transfers between devices, exchange(): lax.all_to_all(block, 'expert', split_axis=0, concat_axis=0, tiled=True)  3.49 us
  transfers between devices with their start and end apart: 19, of which 13 were waited for; matrix products, arithmetic and copies ran while one was open for 1% of the time, Pallas kernels for 5%

profile of v2, /device:TPU:0, one launch (start us, length us, event | category | flops | bytes accessed | tf_op | source)
XLA Modules:
  0.0 116.1 jit_solution(14092539650326878214)
XLA Ops:
  0.6 2.3 %shard_map.129 = (bf16[8,64,512]{2,1,0:T(8,128)(2,1)S(1)}, bf16[128,192]{1,0:T(8,128)(2,1)S(1)}, bf16[1,768,1024]{2,1,0:T(8,128)(2,1)S(1)}) custom-call(s32[8]{0:T(128)} %order.3, bf16[1,768,1024]{2,1,0:T(8,128)(2,1)} %up_hbm.1, bf16[192,2048]{1,0:T(8,128)(2,1)} %tokens_hbm.1, s32[8,192]{1,0:T(8,128)} %bitcast.2), custom_call_target="tpu_custom_call" | custom-call | flops 50331648 | bytes 2365472 | tf_op jit(solution)/shard_map/pallas_call | solution.py:44
  2.9 21.6 %all_to_all.15.own = bf16[8,64,512]{2,1,0:T(8,128)(2,1)S(1)} all-to-all(bf16[8,64,512]{2,1,0:T(8,128)(2,1)S(1)} %get-tuple-element.28), channel_id=1, replica_groups=mesh['expert'=8,'replica'=2,'group'=2] {'expert'}, dimensions={0} | all-to-all | bytes 1048576 | tf_op jit(solution)/shard_map/all_to_all | solution.py:30
  24.6 0.0 copy-start.2
  24.6 0.0 collective-permute-start
  24.6 1.9 %collective-permute-done.other = bf16[8,64,512]{2,1,0:T(8,128)(2,1)S(1)} collective-permute-done((bf16[8,64,512]{2,1,0:T(8,128)(2,1)S(1)}, bf16[8,64,512]{2,1,0:T(8,128)(2,1)S(1)}, u32[]{:S(2)}, u32[]{:S(2)}) %collective-permute-start) | collective-permute-done | bytes 524320 | tf_op jit(solution)/shard_map/ppermute | solution.py:19
  26.5 4.7 %shard_map.133 = (f32[2,64,768]{2,1,0:T(8,128)S(1)}, bf16[2,64,768]{2,1,0:T(8,128)(2,1)S(1)}) custom-call(bf16[1,768,2048]{2,1,0:T(8,128)(2,1)} %gate.3, bf16[1,768,2048]{2,1,0:T(8,128)(2,1)} %up.1, bf16[8,64,512]{2,1,0:T(8,128)(2,1)S(1)} %all_to_all.15.own, bf16[8,64,512]{2,1,0:T(8,128)(2,1)S(1)} %collective-permute-done.other), custom_call_target="tpu_custom_call" | custom-call | flops 805306368 | bytes 7340032 | tf_op jit(solution)/shard_map/pallas_call | solution.py:44
  31.2 1.6 %collective-permute-start.8 = (bf16[2,64,768]{2,1,0:T(8,128)(2,1)S(1)}, bf16[2,64,768]{2,1,0:T(8,128)(2,1)S(1)}, u32[]{:S(2)}, u32[]{:S(2)}) collective-permute-start(bf16[2,64,768]{2,1,0:T(8,128)(2,1)S(1)} %get-tuple-element.38), channel_id=1, source_target_pairs={{0,1},{1,0},{2,3},{3,2},{4,5},{5,4},{6,7},{7,6},{8,9},{9,8},{10,11... | collective-permute-start | bytes 589832 | tf_op jit(solution)/shard_map/ppermute | solution.py:19
  32.8 0.0 copy-done.2
  32.8 0.0 copy-start.1
  32.8 1.1 shard_map.130
  33.9 1.4 %collective-permute-start.1 = (bf16[2,64,768]{2,1,0:T(8,128)(2,1)S(1)}, bf16[2,64,768]{2,1,0:T(8,128)(2,1)S(1)}, u32[]{:S(2)}, u32[]{:S(2)}) collective-permute-start(bf16[2,64,768]{2,1,0:T(8,128)(2,1)S(1)} %get-tuple-element.31), channel_id=1, source_target_pairs={{0,5},{1,4},{4,1},{5,0},{8,13},{9,12},{12,9},{13,8},{16,21},{17,20... | collective-permute-start | bytes 589832 | tf_op jit(solution)/shard_map/ppermute | solution.py:25
  35.3 1.5 %collective-permute-start.2 = (bf16[2,64,768]{2,1,0:T(8,128)(2,1)S(1)}, bf16[2,64,768]{2,1,0:T(8,128)(2,1)S(1)}, u32[]{:S(2)}, u32[]{:S(2)}) collective-permute-start(bf16[2,64,768]{2,1,0:T(8,128)(2,1)S(1)} %get-tuple-element.32), channel_id=1, source_target_pairs={{0,1},{1,0},{2,3},{3,2},{4,5},{5,4},{6,7},{7,6},{8,9},{9,8},{10,11... | collective-permute-start | bytes 589832 | tf_op jit(solution)/shard_map/ppermute | solution.py:19
  36.8 0.6 collective-permute-start.3
  37.4 1.6 %collective-permute-done.8.got = bf16[2,64,768]{2,1,0:T(8,128)(2,1)S(1)} collective-permute-done((bf16[2,64,768]{2,1,0:T(8,128)(2,1)S(1)}, bf16[2,64,768]{2,1,0:T(8,128)(2,1)S(1)}, u32[]{:S(2)}, u32[]{:S(2)}) %collective-permute-start.8) | collective-permute-done | bytes 196640 | tf_op jit(solution)/shard_map/ppermute | solution.py:19
  39.1 0.1 shard_map.134.own
  39.1 1.6 %collective-permute-start.9 = (bf16[64,768]{1,0:T(8,128)(2,1)S(1)}, bf16[64,768]{1,0:T(8,128)(2,1)S(1)}, u32[]{:S(2)}, u32[]{:S(2)}) collective-permute-start(bf16[64,768]{1,0:T(8,128)(2,1)S(1)} %shard_map.134.own), channel_id=1, source_target_pairs={{0,1},{1,0},{2,3},{3,2},{4,5},{5,4},{6,7},{7,6},{8,9},{9,8},{10,11... | collective-permute-start | bytes 294920 | tf_op jit(solution)/shard_map/ppermute | solution.py:19
  40.7 3.5 %collective-permute-done.1.diagonal = bf16[2,64,768]{2,1,0:T(8,128)(2,1)S(1)} collective-permute-done((bf16[2,64,768]{2,1,0:T(8,128)(2,1)S(1)}, bf16[2,64,768]{2,1,0:T(8,128)(2,1)S(1)}, u32[]{:S(2)}, u32[]{:S(2)}) %collective-permute-start.1) | collective-permute-done | bytes 196640 | tf_op jit(solution)/shard_map/ppermute | solution.py:25
  44.2 3.4 %collective-permute-done.2.group = bf16[2,64,768]{2,1,0:T(8,128)(2,1)S(1)} collective-permute-done((bf16[2,64,768]{2,1,0:T(8,128)(2,1)S(1)}, bf16[2,64,768]{2,1,0:T(8,128)(2,1)S(1)}, u32[]{:S(2)}, u32[]{:S(2)}) %collective-permute-start.2) | collective-permute-done | bytes 196640 | tf_op jit(solution)/shard_map/ppermute | solution.py:19
  47.5 0.0 collective-permute-done.3.expert
  47.5 0.1 shard_map.131
  47.6 0.0 copy-start
  47.7 1.5 %collective-permute-start.6 = (bf16[64,768]{1,0:T(8,128)(2,1)S(1)}, bf16[64,768]{1,0:T(8,128)(2,1)S(1)}, u32[]{:S(2)}, u32[]{:S(2)}) collective-permute-start(bf16[64,768]{1,0:T(8,128)(2,1)S(1)} %get-tuple-element.34.own), channel_id=1, source_target_pairs={{0,4},{4,0},{8,12},{12,8},{16,20},{20,16},{24,28},{28,24},{1,5},{5... | collective-permute-start | bytes 294920 | tf_op jit(solution)/shard_map/ppermute | solution.py:19
  49.1 1.5 %collective-permute-start.5 = (bf16[64,768]{1,0:T(8,128)(2,1)S(1)}, bf16[64,768]{1,0:T(8,128)(2,1)S(1)}, u32[]{:S(2)}, u32[]{:S(2)}) collective-permute-start(bf16[64,768]{1,0:T(8,128)(2,1)S(1)} %get-tuple-element.34.own), channel_id=1, source_target_pairs={{0,1},{1,0},{2,3},{3,2},{4,5},{5,4},{6,7},{7,6},{8,9},{9,8},{10,11... | collective-permute-start | bytes 294920 | tf_op jit(solution)/shard_map/ppermute | solution.py:19
  50.6 0.6 collective-permute-start.4
  51.2 0.0 collective-permute-done.9.got
  51.2 0.0 copy-done.1
  51.2 0.6 shard_map.135
  51.8 0.1 collective-permute-start.10
  51.9 1.5 %collective-permute-done.6.expert = bf16[64,768]{1,0:T(8,128)(2,1)S(1)} collective-permute-done((bf16[64,768]{1,0:T(8,128)(2,1)S(1)}, bf16[64,768]{1,0:T(8,128)(2,1)S(1)}, u32[]{:S(2)}, u32[]{:S(2)}) %collective-permute-start.6) | collective-permute-done | bytes 98336 | tf_op jit(solution)/shard_map/ppermute | solution.py:19
  53.4 0.4 collective-permute-done.5.group
  53.8 2.4 %collective-permute-done.4.diagonal = bf16[64,768]{1,0:T(8,128)(2,1)S(1)} collective-permute-done((bf16[64,768]{1,0:T(8,128)(2,1)S(1)}, bf16[64,768]{1,0:T(8,128)(2,1)S(1)}, u32[]{:S(2)}, u32[]{:S(2)}) %collective-permute-start.4) | collective-permute-done | bytes 98336 | tf_op jit(solution)/shard_map/ppermute | solution.py:25
  56.2 0.0 copy-done
  56.2 0.6 shard_map.132
  56.8 0.1 collective-permute-start.7
  56.8 0.0 collective-permute-done.10.teach_got
  56.9 1.5 %collective-permute-done.7.stud_got = bf16[256,512]{1,0:T(8,128)(2,1)S(1)} collective-permute-done((bf16[256,512]{1,0:T(8,128)(2,1)S(1)}, bf16[256,512]{1,0:T(8,128)(2,1)S(1)}, u32[]{:S(2)}, u32[]{:S(2)}) %collective-permute-start.7) | collective-permute-done | bytes 262176 | tf_op jit(solution)/shard_map/ppermute | solution.py:19
  58.4 0.0 copy-start.3
  58.4 0.9 shard_map.136
  59.3 3.5 %all-to-all-start.1 = ((bf16[8,64,512]{2,1,0:T(8,128)(2,1)}), bf16[8,64,512]{2,1,0:T(8,128)(2,1)S(1)}, u32[]{:S(2)}, u32[]{:S(2)}) async-start(bf16[8,64,512]{2,1,0:T(8,128)(2,1)} %shard_map.136), calls=%async_computation.1 | async-start | bytes 1048576 | tf_op jit(solution)/shard_map/all_to_all | solution.py:30
  62.8 0.0 copy-done.3
  62.8 0.0 copy-done.4
  62.8 0.2 shard_map.137.weight
  63.0 14.8 %all-to-all-done.1.back = bf16[8,64,512]{2,1,0:T(8,128)(2,1)S(1)} async-done(((bf16[8,64,512]{2,1,0:T(8,128)(2,1)}), bf16[8,64,512]{2,1,0:T(8,128)(2,1)S(1)}, u32[]{:S(2)}, u32[]{:S(2)}) %all-to-all-start.1) | async-done | bytes 524320 | tf_op jit(solution)/shard_map/all_to_all | solution.py:30
  77.7 1.4 %shard_map.138 = (f32[192,1024]{1,0:T(8,128)S(1)}, bf16[8,32,512]{2,1,0:T(8,128)(2,1)S(1)}) custom-call(s32[8]{0:T(128)} %order.3, bf16[8,64,512]{2,1,0:T(8,128)(2,1)S(1)} %all-to-all-done.1.back, bf16[128,192]{1,0:T(8,128)(2,1)S(1)} %get-tuple-element.41.select, f32[128,1]{1,0:T(8,128)S(1)} %shard_map.137.weight), custom_call_target="tpu_custom_call" | custom-call | flops 201326592 | bytes 573984 | tf_op jit(solution)/shard_map/pallas_call | solution.py:44
  79.1 12.5 %all_to_all.16.own = bf16[8,32,512]{2,1,0:T(8,128)(2,1)S(1)} all-to-all(bf16[8,32,512]{2,1,0:T(8,128)(2,1)S(1)} %get-tuple-element.44), channel_id=1, replica_groups=mesh['expert'=8,'replica'=2,'group'=2] {'expert'}, dimensions={0} | all-to-all | bytes 524288 | tf_op jit(solution)/shard_map/all_to_all | solution.py:30
  91.7 0.0 collective-permute-start.13
  91.7 1.4 %collective-permute-start.11 = (bf16[2,64,768]{2,1,0:T(8,128)(2,1)S(1)}, bf16[2,64,768]{2,1,0:T(8,128)(2,1)S(1)}, u32[]{:S(2)}, u32[]{:S(2)}) collective-permute-start(bf16[2,64,768]{2,1,0:T(8,128)(2,1)S(1)} %get-tuple-element.43.own), channel_id=1, source_target_pairs={{0,4},{4,0},{8,12},{12,8},{16,20},{20,16},{24,28},{28,24},{1,5},{5... | collective-permute-start | bytes 589832 | tf_op jit(solution)/shard_map/ppermute | solution.py:19
  93.1 0.1 collective-permute-done.13.other
  93.2 0.6 shard_map.141
  93.8 0.6 collective-permute-start.14
  94.4 4.6 %collective-permute-done.11.got = bf16[2,64,768]{2,1,0:T(8,128)(2,1)S(1)} collective-permute-done((bf16[2,64,768]{2,1,0:T(8,128)(2,1)S(1)}, bf16[2,64,768]{2,1,0:T(8,128)(2,1)S(1)}, u32[]{:S(2)}, u32[]{:S(2)}) %collective-permute-start.11) | collective-permute-done | bytes 196640 | tf_op jit(solution)/shard_map/ppermute | solution.py:19
  99.0 0.6 collective-permute-start.12
  99.6 1.4 %collective-permute-start.16 = (bf16[128,768]{1,0:T(8,128)(2,1)S(1)}, bf16[128,768]{1,0:T(8,128)(2,1)S(1)}, u32[]{:S(2)}, u32[]{:S(2)}) collective-permute-start(bf16[128,768]{1,0:T(8,128)(2,1)S(1)} %get-tuple-element.46), channel_id=1, source_target_pairs={{0,4},{4,0},{8,12},{12,8},{16,20},{20,16},{24,28},{28,24},{1,5},{5... | collective-permute-start | bytes 589832 | tf_op jit(solution)/shard_map/ppermute | solution.py:19
  101.0 0.0 collective-permute-done.14
  101.1 1.3 %collective-permute-start.15 = (bf16[128,768]{1,0:T(8,128)(2,1)S(1)}, bf16[128,768]{1,0:T(8,128)(2,1)S(1)}, u32[]{:S(2)}, u32[]{:S(2)}) collective-permute-start(bf16[128,768]{1,0:T(8,128)(2,1)S(1)} %add_convert_fusion.1.a_own), channel_id=1, source_target_pairs={{0,4},{4,0},{8,12},{12,8},{16,20},{20,16},{24,28},{28,24},{1,5},{5... | collective-permute-start | bytes 589832 | tf_op jit(solution)/shard_map/ppermute | solution.py:19
  102.4 5.0 %collective-permute-done.16 = bf16[128,768]{1,0:T(8,128)(2,1)S(1)} collective-permute-done((bf16[128,768]{1,0:T(8,128)(2,1)S(1)}, bf16[128,768]{1,0:T(8,128)(2,1)S(1)}, u32[]{:S(2)}, u32[]{:S(2)}) %collective-permute-start.16) | collective-permute-done | bytes 196640 | tf_op jit(solution)/shard_map/ppermute | solution.py:19
  107.4 1.6 %collective-permute-start.17 = (bf16[128,768]{1,0:T(8,128)(2,1)S(1)}, bf16[128,768]{1,0:T(8,128)(2,1)S(1)}, u32[]{:S(2)}, u32[]{:S(2)}) collective-permute-start(bf16[128,768]{1,0:T(8,128)(2,1)S(1)} %add_convert_fusion.b_own), channel_id=1, source_target_pairs={{0,1},{1,0},{2,3},{3,2},{4,5},{5,4},{6,7},{7,6},{8,9},{9,8},{10,11... | collective-permute-start | bytes 589832 | tf_op jit(solution)/shard_map/ppermute | solution.py:19
  109.0 2.1 %collective-permute-done.12.got = bf16[2,128,768]{2,1,0:T(8,128)(2,1)S(1)} collective-permute-done((bf16[2,128,768]{2,1,0:T(8,128)(2,1)S(1)}, bf16[2,128,768]{2,1,0:T(8,128)(2,1)S(1)}, u32[]{:S(2)}, u32[]{:S(2)}) %collective-permute-start.12) | collective-permute-done | bytes 393248 | tf_op jit(solution)/shard_map/ppermute | solution.py:19
  111.1 0.3 shard_map.140.slope
  111.4 0.9 copy.14
  112.3 1.7 %shard_map.143 = bf16[1,768,1024]{2,1,0:T(8,128)(2,1)} custom-call(bf16[256,768]{1,0:T(8,128)(2,1)S(1)} %get-tuple-element.50.hidden, bf16[256,1024]{1,0:T(8,128)(2,1)S(1)} %get-tuple-element.51.rows), custom_call_target="tpu_custom_call" | custom-call | flops 402653184 | bytes 917504 | tf_op jit(solution)/shard_map/pallas_call | solution.py:44
  114.0 0.0 collective-permute-done.15.a_got
  114.0 0.0 collective-permute-done.17.b_got
  114.0 2.1 %shard_map.142 = (bf16[1,768,1024]{2,1,0:T(8,128)(2,1)}, bf16[1,768,1024]{2,1,0:T(8,128)(2,1)}) custom-call(f32[2,256,768]{2,1,0:T(8,128)S(1)} %shard_map.140.slope, bf16[128,768]{1,0:T(8,128)(2,1)S(1)} %add_convert_fusion.1.a_own, bf16[128,768]{1,0:T(8,128)(2,1)S(1)} %collective-permute-done.15.a_got, bf16[128,768]{1,0:T(8,128)(2,1)S(1)} %add_convert_fusion.b_own, ...), custom_call_target="tpu_custom_call" | custom-call | flops 805306368 | bytes 2883584 | tf_op jit(solution)/shard_map/pallas_call | solution.py:44
  (4 shorter events, 0.1 us)
Async XLA Ops:
  24.6 8.2 %copy-start.2 = (bf16[1,768,1024]{2,1,0:T(8,128)(2,1)S(1)}, bf16[1,768,1024]{2,1,0:T(8,128)(2,1)}, u32[]{:S(2)}) copy-start(bf16[1,768,1024]{2,1,0:T(8,128)(2,1)} %gate.2) | copy-start | bytes 4718596
  24.6 1.9 %collective-permute-start = (bf16[8,64,512]{2,1,0:T(8,128)(2,1)S(1)}, bf16[8,64,512]{2,1,0:T(8,128)(2,1)S(1)}, u32[]{:S(2)}, u32[]{:S(2)}) collective-permute-start(bf16[8,64,512]{2,1,0:T(8,128)(2,1)S(1)} %all_to_all.15.own), channel_id=1, source_target_pairs={{0,2},{2,0},{1,3},{3,1},{4,6},{6,4},{5,7},{7,5},{8,10},{10,8},{9,1... | collective-permute-start | bytes 1572872 | tf_op jit(solution)/shard_map/ppermute | solution.py:19
  31.2 7.8 %collective-permute-start.8 = (bf16[2,64,768]{2,1,0:T(8,128)(2,1)S(1)}, bf16[2,64,768]{2,1,0:T(8,128)(2,1)S(1)}, u32[]{:S(2)}, u32[]{:S(2)}) collective-permute-start(bf16[2,64,768]{2,1,0:T(8,128)(2,1)S(1)} %get-tuple-element.38), channel_id=1, source_target_pairs={{0,1},{1,0},{2,3},{3,2},{4,5},{5,4},{6,7},{7,6},{8,9},{9,8},{10,11... | collective-permute-start | bytes 589832 | tf_op jit(solution)/shard_map/ppermute | solution.py:19
  32.8 18.4 %copy-start.1 = (bf16[1,768,2048]{2,1,0:T(8,128)(2,1)S(1)}, bf16[1,768,2048]{2,1,0:T(8,128)(2,1)}, u32[]{:S(2)}) copy-start(bf16[1,768,2048]{2,1,0:T(8,128)(2,1)} %down.4) | copy-start | bytes 9437188
  33.9 10.3 %collective-permute-start.1 = (bf16[2,64,768]{2,1,0:T(8,128)(2,1)S(1)}, bf16[2,64,768]{2,1,0:T(8,128)(2,1)S(1)}, u32[]{:S(2)}, u32[]{:S(2)}) collective-permute-start(bf16[2,64,768]{2,1,0:T(8,128)(2,1)S(1)} %get-tuple-element.31), channel_id=1, source_target_pairs={{0,5},{1,4},{4,1},{5,0},{8,13},{9,12},{12,9},{13,8},{16,21},{17,20... | collective-permute-start | bytes 589832 | tf_op jit(solution)/shard_map/ppermute | solution.py:25
  35.3 12.2 %collective-permute-start.2 = (bf16[2,64,768]{2,1,0:T(8,128)(2,1)S(1)}, bf16[2,64,768]{2,1,0:T(8,128)(2,1)S(1)}, u32[]{:S(2)}, u32[]{:S(2)}) collective-permute-start(bf16[2,64,768]{2,1,0:T(8,128)(2,1)S(1)} %get-tuple-element.32), channel_id=1, source_target_pairs={{0,1},{1,0},{2,3},{3,2},{4,5},{5,4},{6,7},{7,6},{8,9},{9,8},{10,11... | collective-permute-start | bytes 589832 | tf_op jit(solution)/shard_map/ppermute | solution.py:19
  36.8 10.7 %collective-permute-start.3 = (bf16[2,64,768]{2,1,0:T(8,128)(2,1)S(1)}, bf16[2,64,768]{2,1,0:T(8,128)(2,1)S(1)}, u32[]{:S(2)}, u32[]{:S(2)}) collective-permute-start(bf16[2,64,768]{2,1,0:T(8,128)(2,1)S(1)} %get-tuple-element.33), channel_id=1, source_target_pairs={{0,4},{4,0},{8,12},{12,8},{16,20},{20,16},{24,28},{28,24},{1,5},{5... | collective-permute-start | bytes 589832 | tf_op jit(solution)/shard_map/ppermute | solution.py:19
  39.1 12.1 %collective-permute-start.9 = (bf16[64,768]{1,0:T(8,128)(2,1)S(1)}, bf16[64,768]{1,0:T(8,128)(2,1)S(1)}, u32[]{:S(2)}, u32[]{:S(2)}) collective-permute-start(bf16[64,768]{1,0:T(8,128)(2,1)S(1)} %shard_map.134.own), channel_id=1, source_target_pairs={{0,1},{1,0},{2,3},{3,2},{4,5},{5,4},{6,7},{7,6},{8,9},{9,8},{10,11... | collective-permute-start | bytes 294920 | tf_op jit(solution)/shard_map/ppermute | solution.py:19
  47.6 8.5 %copy-start = (bf16[1,768,1024]{2,1,0:T(8,128)(2,1)S(1)}, bf16[1,768,1024]{2,1,0:T(8,128)(2,1)}, u32[]{:S(2)}) copy-start(bf16[1,768,1024]{2,1,0:T(8,128)(2,1)} %down.5) | copy-start | bytes 4718596
  47.7 5.7 %collective-permute-start.6 = (bf16[64,768]{1,0:T(8,128)(2,1)S(1)}, bf16[64,768]{1,0:T(8,128)(2,1)S(1)}, u32[]{:S(2)}, u32[]{:S(2)}) collective-permute-start(bf16[64,768]{1,0:T(8,128)(2,1)S(1)} %get-tuple-element.34.own), channel_id=1, source_target_pairs={{0,4},{4,0},{8,12},{12,8},{16,20},{20,16},{24,28},{28,24},{1,5},{5... | collective-permute-start | bytes 294920 | tf_op jit(solution)/shard_map/ppermute | solution.py:19
  49.1 4.6 %collective-permute-start.5 = (bf16[64,768]{1,0:T(8,128)(2,1)S(1)}, bf16[64,768]{1,0:T(8,128)(2,1)S(1)}, u32[]{:S(2)}, u32[]{:S(2)}) collective-permute-start(bf16[64,768]{1,0:T(8,128)(2,1)S(1)} %get-tuple-element.34.own), channel_id=1, source_target_pairs={{0,1},{1,0},{2,3},{3,2},{4,5},{5,4},{6,7},{7,6},{8,9},{9,8},{10,11... | collective-permute-start | bytes 294920 | tf_op jit(solution)/shard_map/ppermute | solution.py:19
  50.6 5.5 %collective-permute-start.4 = (bf16[64,768]{1,0:T(8,128)(2,1)S(1)}, bf16[64,768]{1,0:T(8,128)(2,1)S(1)}, u32[]{:S(2)}, u32[]{:S(2)}) collective-permute-start(bf16[64,768]{1,0:T(8,128)(2,1)S(1)} %get-tuple-element.34.own), channel_id=1, source_target_pairs={{0,5},{1,4},{4,1},{5,0},{8,13},{9,12},{12,9},{13,8},{16,21},{17,20... | collective-permute-start | bytes 294920 | tf_op jit(solution)/shard_map/ppermute | solution.py:25
  51.8 5.0 %collective-permute-start.10 = (bf16[128,1024]{1,0:T(8,128)(2,1)S(1)}, bf16[128,1024]{1,0:T(8,128)(2,1)S(1)}, u32[]{:S(2)}, u32[]{:S(2)}) collective-permute-start(bf16[128,1024]{1,0:T(8,128)(2,1)S(1)} %get-tuple-element.40), channel_id=1, source_target_pairs={{0,2},{2,0},{1,3},{3,1},{4,6},{6,4},{5,7},{7,5},{8,10},{10,8},{9,1... | collective-permute-start | bytes 786440 | tf_op jit(solution)/shard_map/ppermute | solution.py:19
  56.8 1.6 %collective-permute-start.7 = (bf16[256,512]{1,0:T(8,128)(2,1)S(1)}, bf16[256,512]{1,0:T(8,128)(2,1)S(1)}, u32[]{:S(2)}, u32[]{:S(2)}) collective-permute-start(bf16[256,512]{1,0:T(8,128)(2,1)S(1)} %get-tuple-element.36), channel_id=1, source_target_pairs={{0,2},{2,0},{1,3},{3,1},{4,6},{6,4},{5,7},{7,5},{8,10},{10,8},{9,1... | collective-permute-start | bytes 786440 | tf_op jit(solution)/shard_map/ppermute | solution.py:19
  58.4 4.4 %copy-start.3 = (s32[192,8]{0,1:T(8,128)S(1)}, s32[192,8]{0,1:T(8,128)}, u32[]{:S(2)}) copy-start(s32[192,8]{0,1:T(8,128)} %param.11) | copy-start | bytes 18436
  58.4 4.4 %copy-start.4 = (f32[192,8]{0,1:T(8,128)S(1)}, f32[192,8]{0,1:T(8,128)}, u32[]{:S(2)}) copy-start(f32[192,8]{0,1:T(8,128)} %param.12) | copy-start | bytes 18436
  59.3 18.5 %all-to-all-start.1 = ((bf16[8,64,512]{2,1,0:T(8,128)(2,1)}), bf16[8,64,512]{2,1,0:T(8,128)(2,1)S(1)}, u32[]{:S(2)}, u32[]{:S(2)}) async-start(bf16[8,64,512]{2,1,0:T(8,128)(2,1)} %shard_map.136), calls=%async_computation.1 | async-start | bytes 1048576 | tf_op jit(solution)/shard_map/all_to_all | solution.py:30
  91.7 1.5 %collective-permute-start.13 = (bf16[8,32,512]{2,1,0:T(8,128)(2,1)S(1)}, bf16[8,32,512]{2,1,0:T(8,128)(2,1)S(1)}, u32[]{:S(2)}, u32[]{:S(2)}) collective-permute-start(bf16[8,32,512]{2,1,0:T(8,128)(2,1)S(1)} %all_to_all.16.own), channel_id=1, source_target_pairs={{0,2},{2,0},{1,3},{3,1},{4,6},{6,4},{5,7},{7,5},{8,10},{10,8},{9,1... | collective-permute-start | bytes 786440 | tf_op jit(solution)/shard_map/ppermute | solution.py:19
  91.7 7.3 %collective-permute-start.11 = (bf16[2,64,768]{2,1,0:T(8,128)(2,1)S(1)}, bf16[2,64,768]{2,1,0:T(8,128)(2,1)S(1)}, u32[]{:S(2)}, u32[]{:S(2)}) collective-permute-start(bf16[2,64,768]{2,1,0:T(8,128)(2,1)S(1)} %get-tuple-element.43.own), channel_id=1, source_target_pairs={{0,4},{4,0},{8,12},{12,8},{16,20},{20,16},{24,28},{28,24},{1,5},{5... | collective-permute-start | bytes 589832 | tf_op jit(solution)/shard_map/ppermute | solution.py:19
  93.8 7.2 %collective-permute-start.14 = (bf16[128,768]{1,0:T(8,128)(2,1)S(1)}, bf16[128,768]{1,0:T(8,128)(2,1)S(1)}, u32[]{:S(2)}, u32[]{:S(2)}) collective-permute-start(bf16[128,768]{1,0:T(8,128)(2,1)S(1)} %get-tuple-element.45), channel_id=1, source_target_pairs={{0,1},{1,0},{2,3},{3,2},{4,5},{5,4},{6,7},{7,6},{8,9},{9,8},{10,11... | collective-permute-start | bytes 589832 | tf_op jit(solution)/shard_map/ppermute | solution.py:19
  99.0 12.1 %collective-permute-start.12 = (bf16[2,128,768]{2,1,0:T(8,128)(2,1)S(1)}, bf16[2,128,768]{2,1,0:T(8,128)(2,1)S(1)}, u32[]{:S(2)}, u32[]{:S(2)}) collective-permute-start(bf16[2,128,768]{2,1,0:T(8,128)(2,1)S(1)} %shard_map.139.both), channel_id=1, source_target_pairs={{0,1},{1,0},{2,3},{3,2},{4,5},{5,4},{6,7},{7,6},{8,9},{9,8},{10,11... | collective-permute-start | bytes 1179656 | tf_op jit(solution)/shard_map/ppermute | solution.py:19
  99.6 7.8 %collective-permute-start.16 = (bf16[128,768]{1,0:T(8,128)(2,1)S(1)}, bf16[128,768]{1,0:T(8,128)(2,1)S(1)}, u32[]{:S(2)}, u32[]{:S(2)}) collective-permute-start(bf16[128,768]{1,0:T(8,128)(2,1)S(1)} %get-tuple-element.46), channel_id=1, source_target_pairs={{0,4},{4,0},{8,12},{12,8},{16,20},{20,16},{24,28},{28,24},{1,5},{5... | collective-permute-start | bytes 589832 | tf_op jit(solution)/shard_map/ppermute | solution.py:19
  101.1 12.9 %collective-permute-start.15 = (bf16[128,768]{1,0:T(8,128)(2,1)S(1)}, bf16[128,768]{1,0:T(8,128)(2,1)S(1)}, u32[]{:S(2)}, u32[]{:S(2)}) collective-permute-start(bf16[128,768]{1,0:T(8,128)(2,1)S(1)} %add_convert_fusion.1.a_own), channel_id=1, source_target_pairs={{0,4},{4,0},{8,12},{12,8},{16,20},{20,16},{24,28},{28,24},{1,5},{5... | collective-permute-start | bytes 589832 | tf_op jit(solution)/shard_map/ppermute | solution.py:19
  107.4 6.6 %collective-permute-start.17 = (bf16[128,768]{1,0:T(8,128)(2,1)S(1)}, bf16[128,768]{1,0:T(8,128)(2,1)S(1)}, u32[]{:S(2)}, u32[]{:S(2)}) collective-permute-start(bf16[128,768]{1,0:T(8,128)(2,1)S(1)} %add_convert_fusion.b_own), channel_id=1, source_target_pairs={{0,1},{1,0},{2,3},{3,2},{4,5},{5,4},{6,7},{7,6},{8,9},{9,8},{10,11... | collective-permute-start | bytes 589832 | tf_op jit(solution)/shard_map/ppermute | solution.py:19
